TPU v7x, 256 devices: a whole 4x4x8 slice. The times are simulated.
256 devices in a mesh: dp: 32 (over y, x, core), mp: 8 (over z).
Axes of the slice: x: 4, y: 4, z: 8, core: 2. Of those that a mesh axis runs over, the one named last changes fastest.
Arguments:
- clean: bfloat16 [128, 256, 1536], P('dp', None, 'mp'), may hold values from -6 to 6
- noise: bfloat16 [128, 256, 1536], P('dp', None, 'mp'), may hold values from -6 to 6
- teacher_first: bfloat16 [128, 256, 1536], P('dp', None, 'mp'), may hold values from -6 to 6
- teacher_second: bfloat16 [128, 256, 1536], P('dp', None, 'mp'), may hold values from -6 to 6
- step_index: int32 [128], P('dp'), may hold values from 8 to 32
- teacher_count: int32 [128], P('dp'), may hold values from 64 to 256
- up_master: float32 [1536, 6144], P('dp', 'mp'), may hold values from -6 to 6
- down_master: float32 [1536, 6144], P('dp', 'mp'), may hold values from -6 to 6
- up_moment: float32 [1536, 6144], P('dp', 'mp'), may hold values from -1.8 to 1.8
- down_moment: float32 [1536, 6144], P('dp', 'mp'), may hold values from -1.8 to 1.8
- up_second: float32 [1536, 6144], P('dp', 'mp'), may hold values from 0.002 to 0.032
- down_second: float32 [1536, 6144], P('dp', 'mp'), may hold values from 0.002 to 0.032
Outputs:
- new_up_master: float32 [1536, 6144], P('dp', 'mp')
- new_down_master: float32 [1536, 6144], P('dp', 'mp')
- new_up_moment: float32 [1536, 6144], P('dp', 'mp')
- new_down_moment: float32 [1536, 6144], P('dp', 'mp')
- new_up_second: float32 [1536, 6144], P('dp', 'mp')
- new_down_second: float32 [1536, 6144], P('dp', 'mp')
- loss_mean: float32 [], replicated
Inputs may be any that keep to these rules, and one draw needn't show every extreme that they name: `step_index`: student step k with 2k at most the sample's teacher_count.
All inputs are finite; a program needn't handle non-finite values.
Results may differ from a plain program's by a relative error of at most 0.002.
Values may be sent and summed in bfloat16 or wider, within the bound.
No kernel may reach another device: no remote copies, remote signals or barrier semaphores. Data moves between devices by JAX's collectives and lax.ppermute only.
A program may use at most 64 MiB of HBM per device.

v0:
```python
import math

import jax
import jax.numpy as jnp
from jax import lax
from jax.sharding import Mesh
from jax.sharding import PartitionSpec as P


DP = ("y", "x", "c")
DP_MP = ("y", "x", "c", "mp")


adam_count = 100.0
learn_rate = 0.05
decay_rate = 0.01


PLANE = ("y", "x")


def core_swapped(block):
    return lax.ppermute(block, "c", [(0, 1), (1, 0)])


def core_joined(mine, other):
    first = lax.axis_index("c") == 0
    pair = jnp.where(first, jnp.stack([mine, other], 1), jnp.stack([other, mine], 1))
    return pair.reshape(-1, mine.shape[-1])


def gathered_weights(up_rows, down_rows):
    chips = lax.axis_size(PLANE)
    rows = up_rows.shape[0]
    both = jnp.concatenate([up_rows, down_rows], axis=0)
    mine = lax.all_to_all(
        jnp.broadcast_to(both, (chips,) + both.shape), PLANE, split_axis=0, concat_axis=0, tiled=True
    )
    other = core_swapped(mine)
    return (
        core_joined(mine[:, :rows], other[:, :rows]),
        core_joined(mine[:, rows:], other[:, rows:]),
    )


def core_split(gradient):
    rows = gradient.shape[0] // lax.axis_size(DP)
    core = lax.axis_index("c")
    split = gradient.reshape(lax.axis_size(PLANE), 2, rows, -1)
    sent = lax.dynamic_index_in_dim(split, 1 - core, 1, keepdims=False).astype(jnp.bfloat16)
    return sent, lax.dynamic_index_in_dim(split, core, 1, keepdims=False)


def chip_added(kept, other):
    return (kept + other.astype(jnp.float32)).astype(jnp.bfloat16)


def plane_parts(chip_sum):
    return lax.all_to_all(chip_sum, PLANE, split_axis=0, concat_axis=0, tiled=True)


def added(parts):
    return jnp.sum(parts.astype(jnp.float32), axis=0)


def totals(values):
    devices = lax.axis_size(DP_MP)
    row = jnp.zeros((1, 128), jnp.float32)
    for at, value in enumerate(values):
        row = row.at[0, at].set(value)
    rows = lax.all_to_all(
        jnp.broadcast_to(row, (devices, 128)), DP_MP, split_axis=0, concat_axis=0, tiled=True
    )
    summed = jnp.sum(rows, axis=0)
    return tuple(summed[at] for at in range(len(values)))


def gelu_pair(preact):
    tanh_arg = 0.7978845608028654 * (preact + 0.044715 * preact * preact * preact)
    tanh_val = jnp.tanh(tanh_arg)
    activation = 0.5 * preact * (1.0 + tanh_val)
    slopes = 0.5 * (1.0 + tanh_val) + 0.5 * preact * (
        1.0 - tanh_val * tanh_val
    ) * 0.7978845608028654 * (1.0 + 3.0 * 0.044715 * preact * preact)
    return (activation, slopes)


def distill_target(clean, noise, teacher_first, teacher_second, step_index, teacher_count):
    steps_float = teacher_count.astype(jnp.float32)[:, None, None]
    doubled = 2.0 * step_index.astype(jnp.float32)[:, None, None]
    quarter_turn = 0.5 * math.pi
    time_now = doubled / steps_float
    time_mid = (doubled - 1.0) / steps_float
    time_end = (doubled - 2.0) / steps_float
    alpha_now = jnp.cos(quarter_turn * time_now)
    sigma_now = jnp.sin(quarter_turn * time_now)
    alpha_mid = jnp.cos(quarter_turn * time_mid)
    sigma_mid = jnp.sin(quarter_turn * time_mid)
    alpha_end = jnp.cos(quarter_turn * time_end)
    sigma_end = jnp.sin(quarter_turn * time_end)
    first_f = teacher_first.astype(jnp.float32)
    second_f = teacher_second.astype(jnp.float32)
    latent_now = alpha_now * clean.astype(jnp.float32) + sigma_now * noise.astype(jnp.float32)
    noise_now = (latent_now - alpha_now * first_f) / sigma_now
    latent_mid = alpha_mid * first_f + sigma_mid * noise_now
    noise_mid = (latent_mid - alpha_mid * second_f) / sigma_mid
    latent_end = alpha_end * second_f + sigma_end * noise_mid
    sigma_ratio = sigma_end / sigma_now
    target = (latent_end - sigma_ratio * latent_now) / (alpha_end - sigma_ratio * alpha_now)
    weighting = jnp.maximum(alpha_now * alpha_now / (sigma_now * sigma_now), 1.0)[:, 0, 0]
    return (latent_now, target, weighting)


def adam_update(master, moment, second, gradient, factor):
    clipped = gradient * factor
    moment_new = 0.9 * moment + 0.1 * clipped
    second_new = 0.999 * second + 0.001 * clipped * clipped
    first_hat = moment_new / (1.0 - 0.9**adam_count)
    second_hat = second_new / (1.0 - 0.999**adam_count)
    master_new = master - learn_rate * (
        first_hat / (jnp.sqrt(second_hat) + 1e-08) + decay_rate * master
    )
    return (master_new, moment_new, second_new)


def per_device(
    clean,
    noise,
    teacher_first,
    teacher_second,
    step_index,
    teacher_count,
    up_master,
    down_master,
    up_moment,
    down_moment,
    up_second,
    down_second,
):
    samples_dev, token_count, width_local = clean.shape
    sample_total = samples_dev * lax.axis_size(DP)
    row_count = samples_dev * token_count
    latent, target, weighting = distill_target(
        clean, noise, teacher_first, teacher_second, step_index, teacher_count
    )
    noisy_rows = latent.reshape(row_count, width_local).astype(jnp.bfloat16)
    gathered = lax.all_gather(noisy_rows, "mp", axis=1, tiled=True)
    gathered_f = gathered.astype(jnp.float32)
    normed = (
        gathered_f * lax.rsqrt(jnp.mean(gathered_f * gathered_f, axis=1, keepdims=True) + 1e-06)
    ).astype(jnp.bfloat16)
    up_full, down_full = gathered_weights(
        up_master.astype(jnp.bfloat16), down_master.astype(jnp.bfloat16)
    )
    width_full = up_full.shape[0]
    hidden_local = up_full.shape[1]
    dscale = width_full ** (-0.5)
    fscale = (hidden_local * lax.axis_size("mp")) ** (-0.5)
    preact = jnp.dot(normed, up_full, preferred_element_type=jnp.float32) * dscale
    activation, slopes = gelu_pair(preact)
    hidden = activation.astype(jnp.bfloat16)
    partial_value = (
        lax.dot_general(
            hidden, down_full, (((1,), (1,)), ((), ())), preferred_element_type=jnp.float32
        )
        * fscale
    )
    branch = lax.psum_scatter(
        partial_value.astype(jnp.bfloat16), "mp", scatter_dimension=1, tiled=True
    ).astype(jnp.float32)
    errors = latent + branch.reshape(latent.shape) - target
    weight_cube = weighting[:, None, None]
    loss_part = jnp.sum(weight_cube * errors * errors)
    dpred = (
        (2.0 * weight_cube / sample_total * errors)
        .astype(jnp.bfloat16)
        .reshape(row_count, width_local)
    )
    piece = lax.all_gather(dpred, "mp", axis=1, tiled=True)
    grad_piece = (
        lax.dot_general(piece, hidden, (((0,), (0,)), ((), ())), preferred_element_type=jnp.float32)
        * fscale
    )
    sent_down, kept_down = core_split(grad_piece)
    other_down = core_swapped(sent_down)
    piece, sent_down = lax.optimization_barrier((piece, sent_down))
    summed = jnp.dot(piece, down_full, preferred_element_type=jnp.float32)
    dpre = (summed * fscale * slopes).astype(jnp.bfloat16)
    dpre, chip_down = lax.optimization_barrier((dpre, chip_added(kept_down, other_down)))
    parts_down = plane_parts(chip_down)
    grad_up = (
        lax.dot_general(normed, dpre, (((0,), (0,)), ((), ())), preferred_element_type=jnp.float32)
        * dscale
    )
    sent_up, kept_up = core_split(grad_up)
    parts_up = plane_parts(chip_added(kept_up, core_swapped(sent_up)))
    mine_up, mine_down = added(parts_up), added(parts_down)
    squares = jnp.sum(mine_up * mine_up) + jnp.sum(mine_down * mine_down)
    loss_total, square_total = totals((loss_part, squares))
    clip_limit = math.sqrt(2.0 * width_full * hidden_local * lax.axis_size("mp"))
    factor = clip_limit / jnp.maximum(jnp.sqrt(square_total), clip_limit)
    new_up, up_m, up_v = adam_update(up_master, up_moment, up_second, mine_up, factor)
    new_down, down_m, down_v = adam_update(
        down_master, down_moment, down_second, mine_down, factor
    )
    loss_mean = loss_total / (sample_total * token_count * width_full)
    return (new_up, new_down, up_m, down_m, up_v, down_v, loss_mean)


def solution(mesh):
    split = Mesh(mesh.devices.reshape(4, 4, 2, mesh.shape["mp"]), DP_MP)
    placed = (
        P(DP, None, "mp"),
        P(DP, None, "mp"),
        P(DP, None, "mp"),
        P(DP, None, "mp"),
        P(DP),
        P(DP),
        P(DP, "mp"),
        P(DP, "mp"),
        P(DP, "mp"),
        P(DP, "mp"),
        P(DP, "mp"),
        P(DP, "mp"),
    )

    return jax.shard_map(
        per_device,
        mesh=split,
        in_specs=placed,
        out_specs=(
            P(DP, "mp"),
            P(DP, "mp"),
            P(DP, "mp"),
            P(DP, "mp"),
            P(DP, "mp"),
            P(DP, "mp"),
            P(),
        ),
        check_vma=False,
    )
```

profile of v0, /device:TPU:2, one launch (start us, length us, event | category | flops | bytes accessed | tf_op | source)
XLA Modules:
  0.0 278.4 jit_solution(12794395123624888192)
XLA Ops:
  12.8 37.1 %all_to_all.21 = bf16[16,96,768]{2,1,0:T(8,128)(2,1)S(1)} all-to-all(bf16[16,96,768]{2,1,0:T(8,128)(2,1)S(1)} %broadcast_in_dim.4), channel_id=1, replica_groups=mesh['y'=4,'x'=4,'c'=2,'mp'=8] {'y','x'}, dimensions={0} | all-to-all | bytes 4718592 | tf_op jit(solution)/shard_map/all_to_all | solution.py:36
  50.1 4.5 %collective-permute-done = bf16[16,96,768]{2,1,0:T(8,128)(2,1)} collective-permute-done((bf16[16,96,768]{2,1,0:T(8,128)(2,1)S(1)}, bf16[16,96,768]{2,1,0:T(8,128)(2,1)}, u32[]{:S(2)}, u32[]{:S(2)}) %collective-permute-start) | collective-permute-done | bytes 2359328 | tf_op jit(solution)/shard_map/ppermute | solution.py:23
  54.6 1.8 slice_bitcast_fusion
  56.8 1.8 copy.37
  58.6 1.7 maximum_select_fusion
  60.3 2.7 fusion
  63.1 4.5 %fusion.6 = f32[1024,768]{1,0:T(8,128)S(1)} fusion(bf16[1536,768]{1,0:T(8,128)(2,1)} %bitcast.60, bf16[1024,1536]{0,1:T(8,128)(2,1)S(1)} %copy-done, f32[1024]{0:T(1024)S(1)} %add_rsqrt_fusion), kind=kOutput, calls=%fused_computation.13 | convolution fusion | flops 2420637696 | bytes 8654848 | tf_op jit(solution)/shard_map/dot_general | solution.py:159
  69.3 4.4 %multiply_convert_fusion = bf16[1024,1536]{0,1:T(8,128)(2,1)} fusion(bf16[1536,768]{1,0:T(8,128)(2,1)S(1)} %bitcast.59, f32[1024,768]{1,0:T(8,128)S(1)} %fusion.6), kind=kOutput, calls=%fused_computation.4 | convolution fusion | flops 2426929152 | bytes 8650752 | tf_op jit(solution)/shard_map/dot_general | solution.py:163
  76.4 44.4 %reduce-scatter.2.cloned.1.call-done = bf16[1024,192]{0,1:T(8,128)(2,1)} async-done(((bf16[1024,1536]{0,1:T(8,128)(2,1)}), bf16[1024,192]{0,1:T(8,128)(2,1)}) %reduce-scatter.2.cloned.1.call-update) | async-done | bytes 393232 | tf_op jit(solution)/shard_map/reduce_scatter | solution.py:168
  121.9 2.7 fusion.23
  125.6 44.6 %all-gather.5.cloned.1.call-done = bf16[1024,1536]{0,1:T(8,128)(2,1)} async-done(((bf16[1024,192]{0,1:T(8,128)(2,1)}), bf16[1024,1536]{0,1:T(8,128)(2,1)}) %all-gather.5.cloned.1.call-update) | async-done | bytes 3145744 | tf_op jit(solution)/shard_map/all_gather | solution.py:179
  170.2 5.7 %convolution_multiply_fusion.1 = f32[1536,768]{1,0:T(8,128)S(1)} fusion(bf16[1024,1536]{0,1:T(8,128)(2,1)} %all-gather.5.cloned.1.call-done, f32[1024,768]{1,0:T(8,128)} %copy-done.14), kind=kOutput, calls=%fused_computation.7 | convolution fusion | flops 2424963072 | bytes 11010048 | tf_op jit(solution)/shard_map/dot_general | solution.py:181
  175.9 2.1 copy-done.1
  179.2 8.1 %multiply_convert_fusion.1 = bf16[1024,768]{1,0:T(8,128)(2,1)S(1)} fusion(f32[1024,768]{1,0:T(8,128)} %copy-done.14, bf16[1024,1536]{0,1:T(8,128)(2,1)} %all-gather.5.cloned.1.call-done, bf16[1536,768]{1,0:T(8,128)(2,1)} %bitcast.58), kind=kOutput, calls=%fused_computation.10 | convolution fusion | flops 2432434176 | bytes 10223616 | tf_op jit(solution)/shard_map/dot_general | solution.py:187
  187.3 2.7 fusion.9
  190.0 2.7 convolution_multiply_fusion
  192.7 2.1 copy-done.3
  195.7 7.3 %all-to-all-start.2 = ((bf16[16,48,768]{2,1,0:T(8,128)(2,1)}), bf16[16,48,768]{2,1,0:T(8,128)(2,1)S(1)}, u32[]{:S(2)}, u32[]{:S(2)}) async-start(bf16[16,48,768]{2,1,0:T(8,128)(2,1)} %fusion.9), calls=%async_computation.3 | async-start | bytes 2359296 | tf_op jit(solution)/shard_map/all_to_all | solution.py:59
  203.0 3.0 %fusion.8 = bf16[16,48,768]{2,1,0:T(8,128)(2,1)} fusion(bf16[16,48,768]{2,1,0:T(8,128)(2,1)S(1)} %collective-permute-done.2, f32[16,2,48,768]{3,2,1,0:T(8,128)} %bitcast.57, s32[]{:T(128)S(6)} %select_n.35), kind=kLoop, calls=%fused_computation.17 | loop fusion | flops 1769472 | bytes 4718596 | tf_op jit(solution)/shard_map/convert_element_type | solution.py:55
  206.0 14.3 %all-to-all-done.2 = bf16[16,48,768]{2,1,0:T(8,128)(2,1)S(1)} async-done(((bf16[16,48,768]{2,1,0:T(8,128)(2,1)}), bf16[16,48,768]{2,1,0:T(8,128)(2,1)S(1)}, u32[]{:S(2)}, u32[]{:S(2)}) %all-to-all-start.2) | async-done | bytes 1179680 | tf_op jit(solution)/shard_map/all_to_all | solution.py:59
  220.4 5.7 %all-to-all-start.1 = ((bf16[16,48,768]{2,1,0:T(8,128)(2,1)}), bf16[16,48,768]{2,1,0:T(8,128)(2,1)S(1)}, u32[]{:S(2)}, u32[]{:S(2)}) async-start(bf16[16,48,768]{2,1,0:T(8,128)(2,1)} %fusion.8), calls=%async_computation.2 | async-start | bytes 2359296 | tf_op jit(solution)/shard_map/all_to_all | solution.py:59
  230.0 13.0 %all-to-all-done.1 = bf16[16,48,768]{2,1,0:T(8,128)(2,1)S(1)} async-done(((bf16[16,48,768]{2,1,0:T(8,128)(2,1)}), bf16[16,48,768]{2,1,0:T(8,128)(2,1)S(1)}, u32[]{:S(2)}, u32[]{:S(2)}) %all-to-all-start.1) | async-done | bytes 1179680 | tf_op jit(solution)/shard_map/all_to_all | solution.py:59
  245.1 1.9 fusion.44
  248.4 19.2 %all_to_all.22 = f32[256,1,128]{2,1,0:T(1,128)S(1)} all-to-all(f32[256,1,128]{2,1,0:T(1,128)S(1)} %broadcast_in_dim.5), channel_id=1, replica_groups=mesh['y'=4,'x'=4,'c'=2,'mp'=8] {'y','x','c','mp'}, dimensions={0} | all-to-all | bytes 262144 | tf_op jit(solution)/shard_map/all_to_all | solution.py:71
  (73 shorter events, 21.2 us)
Async XLA Ops:
  7.2 53.1 %all-gather.3.cloned.1.call-start = ((), (), s32[]{:S(2)}) async-start(), calls=%async_computation.5 | async-start | bytes 3538944 | tf_op jit(solution)/shard_map/all_gather | solution.py:147
  10.7 110.1 %reduce-scatter.2.cloned.1.call-start = ((), (), s32[]{:S(2)}) async-start(), calls=%async_computation.6 | async-start | bytes 3538944 | tf_op jit(solution)/shard_map/reduce_scatter | solution.py:168
  49.9 4.7 %collective-permute-start = (bf16[16,96,768]{2,1,0:T(8,128)(2,1)S(1)}, bf16[16,96,768]{2,1,0:T(8,128)(2,1)}, u32[]{:S(2)}, u32[]{:S(2)}) collective-permute-start(bf16[16,96,768]{2,1,0:T(8,128)(2,1)S(1)} %all_to_all.21), channel_id=1, source_target_pairs={{0,8},{8,0},{1,9},{9,1},{2,10},{10,2},{3,11},{11,3},{4,12},{12,4},... | collective-permute-start | bytes 7077896 | tf_op jit(solution)/shard_map/ppermute | solution.py:23
  60.3 2.8 %copy-start = (bf16[1024,1536]{0,1:T(8,128)(2,1)S(1)}, bf16[1024,1536]{0,1:T(8,128)(2,1)}, u32[]{:S(2)}) copy-start(bf16[1024,1536]{0,1:T(8,128)(2,1)} %all-gather.3.cloned.1.call-done) | copy-start | bytes 9437188
  63.1 6.2 %copy-start.4 = (bf16[16,2,48,768]{3,2,1,0:T(8,128)(2,1)S(1)}, bf16[16,2,48,768]{3,2,1,0:T(8,128)(2,1)}, u32[]{:S(2)}) copy-start(bf16[16,2,48,768]{3,2,1,0:T(8,128)(2,1)} %copy.37) | copy-start | bytes 7077892
  67.6 1.6 copy-start.14
  73.7 48.2 %copy-start.5 = (bf16[4,256,192]{1,2,0:T(8,128)(2,1)S(1)}, bf16[4,256,192]{1,2,0:T(8,128)(2,1)}, u32[]{:S(2)}) copy-start(bf16[4,256,192]{1,2,0:T(8,128)(2,1)} %param.17) | copy-start | bytes 1179652
  73.7 96.5 %all-gather.5.cloned.1.call-start = ((), (), s32[]{:S(2)}) async-start(), calls=%async_computation.7 | async-start | bytes 3538944 | tf_op jit(solution)/shard_map/all_gather | solution.py:179
  74.6 1.2 copy-start.12
  120.8 3.8 %copy-start.13 = (f32[4]{0:T(128)S(1)}, f32[4]{0:T(128)}, u32[]{:S(2)}) copy-start(f32[4]{0:T(128)} %get-tuple-element.63) | copy-start | bytes 52
  175.9 2.1 copy-start.1
  179.2 8.1 %collective-permute-start.1 = (bf16[16,48,768]{2,1,0:T(8,128)(2,1)}, bf16[16,48,768]{2,1,0:T(8,128)(2,1)}, u32[]{:S(2)}, u32[]{:S(2)}) collective-permute-start(bf16[16,48,768]{2,1,0:T(8,128)(2,1)} %fusion.10), channel_id=1, source_target_pairs={{0,8},{8,0},{1,9},{9,1},{2,10},{10,2},{3,11},{11,3},{4,12},{12,4},... | collective-permute-start | bytes 3538952 | tf_op jit(solution)/shard_map/ppermute | solution.py:23
  179.2 8.1 %copy-start.2 = (f32[1536,768]{1,0:T(8,128)S(1)}, f32[1536,768]{1,0:T(8,128)}, u32[]{:S(2)}) copy-start(f32[1536,768]{1,0:T(8,128)} %copy-done.1) | copy-start | bytes 14155780
  192.7 2.1 copy-start.3
  194.9 8.1 %collective-permute-start.2 = (bf16[16,48,768]{2,1,0:T(8,128)(2,1)S(1)}, bf16[16,48,768]{2,1,0:T(8,128)(2,1)S(1)}, u32[]{:S(2)}, u32[]{:S(2)}) collective-permute-start(bf16[16,48,768]{2,1,0:T(8,128)(2,1)S(1)} %fusion.11), channel_id=1, source_target_pairs={{0,8},{8,0},{1,9},{9,1},{2,10},{10,2},{3,11},{11,3},{4,12},{12,4},... | collective-permute-start | bytes 3538952 | tf_op jit(solution)/shard_map/ppermute | solution.py:23
  195.7 24.7 %all-to-all-start.2 = ((bf16[16,48,768]{2,1,0:T(8,128)(2,1)}), bf16[16,48,768]{2,1,0:T(8,128)(2,1)S(1)}, u32[]{:S(2)}, u32[]{:S(2)}) async-start(bf16[16,48,768]{2,1,0:T(8,128)(2,1)} %fusion.9), calls=%async_computation.3 | async-start | bytes 2359296 | tf_op jit(solution)/shard_map/all_to_all | solution.py:59
  206.0 63.7 %copy-start.6 = (f32[48,768]{1,0:T(8,128)S(1)}, f32[48,768]{1,0:T(8,128)}, u32[]{:S(2)}) copy-start(f32[48,768]{1,0:T(8,128)} %param.23) | copy-start | bytes 442372
  206.0 63.7 %copy-start.7 = (f32[48,768]{1,0:T(8,128)S(1)}, f32[48,768]{1,0:T(8,128)}, u32[]{:S(2)}) copy-start(f32[48,768]{1,0:T(8,128)} %param.22) | copy-start | bytes 442372
  206.0 63.7 %copy-start.8 = (f32[48,768]{1,0:T(8,128)S(1)}, f32[48,768]{1,0:T(8,128)}, u32[]{:S(2)}) copy-start(f32[48,768]{1,0:T(8,128)} %param.25) | copy-start | bytes 442372
  206.0 63.7 %copy-start.9 = (f32[48,768]{1,0:T(8,128)S(1)}, f32[48,768]{1,0:T(8,128)}, u32[]{:S(2)}) copy-start(f32[48,768]{1,0:T(8,128)} %param.27) | copy-start | bytes 442372
  206.0 63.7 %copy-start.10 = (f32[48,768]{1,0:T(8,128)S(1)}, f32[48,768]{1,0:T(8,128)}, u32[]{:S(2)}) copy-start(f32[48,768]{1,0:T(8,128)} %param.26) | copy-start | bytes 442372
  206.0 63.7 %copy-start.11 = (f32[48,768]{1,0:T(8,128)S(1)}, f32[48,768]{1,0:T(8,128)}, u32[]{:S(2)}) copy-start(f32[48,768]{1,0:T(8,128)} %param.24) | copy-start | bytes 442372
  220.4 22.7 %all-to-all-start.1 = ((bf16[16,48,768]{2,1,0:T(8,128)(2,1)}), bf16[16,48,768]{2,1,0:T(8,128)(2,1)S(1)}, u32[]{:S(2)}, u32[]{:S(2)}) async-start(bf16[16,48,768]{2,1,0:T(8,128)(2,1)} %fusion.8), calls=%async_computation.2 | async-start | bytes 2359296 | tf_op jit(solution)/shard_map/all_to_all | solution.py:59
Sparse Core Ops, SparseCore 0:
  10.8 47.9 all-gather.2
  73.8 46.9 reduce-scatter.1
  125.7 44.3 all-gather.4
where the time goes:
time: 282 us; the launch traced here: 278 us
  waiting for transfers between devices  121 us (43%)
  blocking collectives  56.3 us (20%)
  matrix products  25.4 us (9%)
  other arithmetic  25.3 us (9%)
  between operations  19.1 us (7%)
  local copies, waits for them, and re-layouts  17.3 us (6%)
  starting transfers between devices  14 us (5%)
    all_gather x1, waiting for transfers between devices, per_device(): piece = lax.all_gather(dpred, 'mp', axis=1, tiled=True)  44.6 us
    reduce_scatter x1, waiting for transfers between devices, per_device(): lax.psum_scatter(partial_value.astype(jnp.bfloat16), 'mp', scatter_dimens...  44.4 us
    all_to_all x1, blocking collectives, gathered_weights(): lax.all_to_all(jnp.broadcast_to(both, (chips,) + both.shape), PLANE, spli...  37.1 us
    all_to_all x2, waiting for transfers between devices, plane_parts(): lax.all_to_all(chip_sum, PLANE, split_axis=0, concat_axis=0, tiled=True)  27.4 us
    all_to_all x1, blocking collectives, totals(): lax.all_to_all(jnp.broadcast_to(row, (devices, 128)), DP_MP, split_axis=0...  19.2 us
    all_to_all x2, starting transfers between devices, plane_parts(): lax.all_to_all(chip_sum, PLANE, split_axis=0, concat_axis=0, tiled=True)  12.9 us
    dot_general x1, matrix products, per_device(): summed = jnp.dot(piece, down_full, preferred_element_type=jnp.float32)  8.1 us
    unnamed x30, local copies, waits for them, and re-layouts  6.01 us
  transfers between devices with their start and end apart: 8, of which 5 were waited for; matrix products, arithmetic and copies ran while one was open for 9% of the time, Pallas kernels for 0%

commit v1 on v0

--- a/solution.py
+++ b/solution.py
@@ -5,7 +5,6 @@
 from jax import lax
 from jax.sharding import Mesh
 from jax.sharding import PartitionSpec as P
-
 
 DP = ("y", "x", "c")
 DP_MP = ("y", "x", "c", "mp")
@@ -43,36 +42,23 @@
     )
 
 
-def core_split(gradient):
-    rows = gradient.shape[0] // lax.axis_size(DP)
-    core = lax.axis_index("c")
-    split = gradient.reshape(lax.axis_size(PLANE), 2, rows, -1)
-    sent = lax.dynamic_index_in_dim(split, 1 - core, 1, keepdims=False).astype(jnp.bfloat16)
-    return sent, lax.dynamic_index_in_dim(split, core, 1, keepdims=False)
-
-
-def chip_added(kept, other):
-    return (kept + other.astype(jnp.float32)).astype(jnp.bfloat16)
-
-
-def plane_parts(chip_sum):
-    return lax.all_to_all(chip_sum, PLANE, split_axis=0, concat_axis=0, tiled=True)
-
-
-def added(parts):
-    return jnp.sum(parts.astype(jnp.float32), axis=0)
-
-
-def totals(values):
-    devices = lax.axis_size(DP_MP)
-    row = jnp.zeros((1, 128), jnp.float32)
-    for at, value in enumerate(values):
-        row = row.at[0, at].set(value)
+def half_columns(block, which):
+    half = block.shape[1] // 2
+    return lax.dynamic_slice_in_dim(block, which * half, half, axis=1)
+
+
+def over_tokens(left, right):
+    return lax.dot_general(left, right, (((0,), (0,)), ((), ())), preferred_element_type=jnp.float32)
+
+
+def totals(first, second):
+    shape = (lax.axis_size(DP_MP), 128)
+    lane = lax.broadcasted_iota(jnp.int32, shape, 1)
     rows = lax.all_to_all(
-        jnp.broadcast_to(row, (devices, 128)), DP_MP, split_axis=0, concat_axis=0, tiled=True
+        jnp.where(lane < 64, first, second), DP_MP, split_axis=0, concat_axis=0, tiled=True
     )
     summed = jnp.sum(rows, axis=0)
-    return tuple(summed[at] for at in range(len(values)))
+    return summed[0], summed[64]
 
 
 def gelu_pair(preact):
@@ -159,16 +145,19 @@
     preact = jnp.dot(normed, up_full, preferred_element_type=jnp.float32) * dscale
     activation, slopes = gelu_pair(preact)
     hidden = activation.astype(jnp.bfloat16)
+    core = lax.axis_index("c")
     partial_value = (
         lax.dot_general(
             hidden, down_full, (((1,), (1,)), ((), ())), preferred_element_type=jnp.float32
         )
         * fscale
-    )
-    branch = lax.psum_scatter(
-        partial_value.astype(jnp.bfloat16), "mp", scatter_dimension=1, tiled=True
-    ).astype(jnp.float32)
-    errors = latent + branch.reshape(latent.shape) - target
+    ).astype(jnp.bfloat16)
+    offset = lax.optimization_barrier(latent - target)
+    branch = lax.psum_scatter(partial_value, "mp", scatter_dimension=1, tiled=True).astype(
+        jnp.float32
+    )
+    normed_other, hidden_other = core_swapped(normed), core_swapped(half_columns(hidden, 1 - core))
+    errors = offset + branch.reshape(latent.shape)
     weight_cube = weighting[:, None, None]
     loss_part = jnp.sum(weight_cube * errors * errors)
     dpred = (
@@ -177,26 +166,33 @@
         .reshape(row_count, width_local)
     )
     piece = lax.all_gather(dpred, "mp", axis=1, tiled=True)
-    grad_piece = (
-        lax.dot_general(piece, hidden, (((0,), (0,)), ((), ())), preferred_element_type=jnp.float32)
-        * fscale
-    )
-    sent_down, kept_down = core_split(grad_piece)
-    other_down = core_swapped(sent_down)
-    piece, sent_down = lax.optimization_barrier((piece, sent_down))
+    piece_other = core_swapped(piece)
     summed = jnp.dot(piece, down_full, preferred_element_type=jnp.float32)
     dpre = (summed * fscale * slopes).astype(jnp.bfloat16)
-    dpre, chip_down = lax.optimization_barrier((dpre, chip_added(kept_down, other_down)))
-    parts_down = plane_parts(chip_down)
+    dpre_other = core_swapped(half_columns(dpre, 1 - core))
+    grad_down = (
+        over_tokens(piece, half_columns(hidden, core)) + over_tokens(piece_other, hidden_other)
+    ) * fscale
     grad_up = (
-        lax.dot_general(normed, dpre, (((0,), (0,)), ((), ())), preferred_element_type=jnp.float32)
-        * dscale
-    )
-    sent_up, kept_up = core_split(grad_up)
-    parts_up = plane_parts(chip_added(kept_up, core_swapped(sent_up)))
-    mine_up, mine_down = added(parts_up), added(parts_down)
-    squares = jnp.sum(mine_up * mine_up) + jnp.sum(mine_down * mine_down)
-    loss_total, square_total = totals((loss_part, squares))
+        over_tokens(normed, half_columns(dpre, core)) + over_tokens(normed_other, dpre_other)
+    ) * dscale
+    chips = lax.axis_size(PLANE)
+    rows_chip = width_full // chips
+    halves = [
+        g.astype(jnp.bfloat16).reshape(chips, rows_chip, -1) for g in (grad_up, grad_down)
+    ]
+    parts = lax.all_to_all(
+        jnp.concatenate(halves, axis=1), PLANE, split_axis=0, concat_axis=0, tiled=True
+    )
+    chip_rows = jnp.sum(parts.astype(jnp.float32), axis=0)
+    squares = jnp.sum(chip_rows * chip_rows)
+    loss_total, square_total = totals(loss_part, squares)
+    by_core = chip_rows.reshape(2, 2, rows_chip // 2, -1)
+    kept = lax.dynamic_index_in_dim(by_core, core, 1, keepdims=False)
+    other = core_swapped(lax.dynamic_index_in_dim(by_core, 1 - core, 1, keepdims=False))
+    mine_up, mine_down = jnp.where(
+        core == 0, jnp.concatenate([kept, other], 2), jnp.concatenate([other, kept], 2)
+    )
     clip_limit = math.sqrt(2.0 * width_full * hidden_local * lax.axis_size("mp"))
     factor = clip_limit / jnp.maximum(jnp.sqrt(square_total), clip_limit)
     new_up, up_m, up_v = adam_update(up_master, up_moment, up_second, mine_up, factor)

time: 282 us -> 272 us (0.965)
  waiting for transfers between devices: 121 us -> 141 us
  blocking collectives: 56.3 us -> 37.1 us
  local copies, waits for them, and re-layouts: 17.3 us -> 9.1 us
  other arithmetic: 25.3 us -> 17.8 us
  starting transfers between devices: 14 us -> 20 us
    all_to_all x1 -> x0, blocking collectives: 19.2 us -> none  [totals(): lax.all_to_all(jnp.broadcast_to(row, (devices, 128)), DP_MP, split_axis=0...]
    all_to_all x2, waiting for transfers between devices: 27.4 us -> 44.5 us  [the longest x1 33.2 us: per_device(): lax.all_to_all(jnp.concatenate(halves, axis=1), PLANE, split_axis=0, conc...]
    all_to_all x2, starting transfers between devices: 12.9 us -> 19 us  [the longest x1 11.7 us: totals(): lax.all_to_all(jnp.where(lane < 64, first, second), DP_MP, split_axis=0,...]
    convert_element_type x2 -> x1, other arithmetic: 5.7 us -> 0.9 us  [per_device(): normed = (gathered_f * lax.rsqrt(jnp.mean(gathered_f * gathered_f, axis=1...]
    unnamed x30 -> x24, local copies, waits for them, and re-layouts: 6.01 us -> 2.03 us
    another operation x3 -> x0, other arithmetic: 3.16 us -> none
    dot_general x2 -> x4, matrix products: 8.37 us -> 11 us  [over_tokens(): lax.dot_general(left, right, (((0,), (0,)), ((), ())), preferred_element_...]
  transfers between devices with their start and end apart: 8 -> 11, of which waited for: 5 -> 6; matrix products, arithmetic and copies ran while one was open for 9% -> 9% of each run, Pallas kernels for 0% -> 0%
where the time goes in v1:
time: 272 us; the launch traced here: 269 us
  waiting for transfers between devices  141 us (52%)
  blocking collectives  37.1 us (14%)
  matrix products  28.1 us (10%)
  starting transfers between devices  20 us (7%)
  other arithmetic  17.8 us (7%)
  between operations  16.6 us (6%)
  local copies, waits for them, and re-layouts  9.1 us (3%)
    reduce_scatter x1, waiting for transfers between devices, per_device(): lax.psum_scatter(partial_value, 'mp', scatter_dimension=1, tiled=True)  46.6 us
    all_gather x1, waiting for transfers between devices, per_device(): piece = lax.all_gather(dpred, 'mp', axis=1, tiled=True)  44.6 us
    all_to_all x1, blocking collectives, gathered_weights(): lax.all_to_all(jnp.broadcast_to(both, (chips,) + both.shape), PLANE, spli...  37.1 us
    all_to_all x1, waiting for transfers between devices, per_device(): lax.all_to_all(jnp.concatenate(halves, axis=1), PLANE, split_axis=0, conc...  33.2 us
    all_to_all x1, starting transfers between devices, totals(): lax.all_to_all(jnp.where(lane < 64, first, second), DP_MP, split_axis=0,...  11.7 us
    all_to_all x1, waiting for transfers between devices, totals(): lax.all_to_all(jnp.where(lane < 64, first, second), DP_MP, split_axis=0,...  11.3 us
    dot_general x4, matrix products, over_tokens(): lax.dot_general(left, right, (((0,), (0,)), ((), ())), preferred_element_...  11 us
    dot_general x1, matrix products, per_device(): summed = jnp.dot(piece, down_full, preferred_element_type=jnp.float32)  8.06 us
  transfers between devices with their start and end apart: 11, of which 6 were waited for; matrix products, arithmetic and copies ran while one was open for 9% of the time, Pallas kernels for 0%

profile of v1, /device:TPU:2, one launch (start us, length us, event | category | flops | bytes accessed | tf_op | source)
XLA Modules:
  0.0 269.4 jit_solution(16437615804746110913)
XLA Ops:
  8.2 2.9 %fusion.26 = (bf16[4,24,8,256]{3,2,1,0:T(8,128)(2,1)S(1)}, f32[4,256,192]{1,2,0:T(8,128)}) fusion(bf16[4,256,192]{1,2,0:T(8,128)(2,1)} %param.13, bf16[4,256,192]{1,2,0:T(8,128)(2,1)} %param.12, f32[4]{0:T(128)S(1)} %sin.12, f32[4]{0:T(128)S(1)} %get-tuple-element.38, f32[4]{0:T(128)S(1)} %get-tuple-element.15, f32[4]{0:T(128)S(1)} %get-tuple-element.16, ...), kind=kLoop, calls=%fused_computation.50 | loop fusion | flops 4718592 | bytes 2752640
  12.3 37.1 %all_to_all.16 = bf16[16,96,768]{2,1,0:T(8,128)(2,1)S(1)} all-to-all(bf16[16,96,768]{2,1,0:T(8,128)(2,1)S(1)} %broadcast_in_dim.14), channel_id=1, replica_groups=mesh['y'=4,'x'=4,'c'=2,'mp'=8] {'y','x'}, dimensions={0} | all-to-all | bytes 4718592 | tf_op jit(solution)/shard_map/all_to_all | solution.py:35
  49.6 4.5 %collective-permute-done = bf16[16,96,768]{2,1,0:T(8,128)(2,1)} collective-permute-done((bf16[16,96,768]{2,1,0:T(8,128)(2,1)S(1)}, bf16[16,96,768]{2,1,0:T(8,128)(2,1)}, u32[]{:S(2)}, u32[]{:S(2)}) %collective-permute-start) | collective-permute-done | bytes 2359328 | tf_op jit(solution)/shard_map/ppermute | solution.py:22
  54.1 1.8 slice_bitcast_fusion
  56.3 1.7 copy.37
  58.0 1.6 maximum_select_fusion
  60.1 2.7 %fusion = f32[1024]{0:T(1024)S(1)} fusion(bf16[1024,1536]{0,1:T(8,128)(2,1)} %all-gather.3.cloned.1.call-done), kind=kLoop, calls=%fused_computation.2 | loop fusion | flops 4717568 | bytes 3149824 | tf_op jit(solution)/shard_map/reduce_sum | solution.py:136
  64.6 5.0 %multiply_convert_fusion.2 = (bf16[1024,768]{1,0:T(8,128)(2,1)S(1)}, f32[1024,768]{1,0:T(8,128)}) fusion(bf16[1024,1536]{0,1:T(8,128)(2,1)S(1)} %fusion.1, bf16[1536,768]{1,0:T(8,128)(2,1)S(1)} %bitcast.65), kind=kOutput, calls=%fused_computation.10 | convolution fusion | flops 2423783424 | bytes 10223616 | tf_op jit(solution)/shard_map/dot_general | solution.py:145
  69.6 1.2 copy-done.5
  70.7 4.0 %multiply_convert_fusion = bf16[1024,1536]{0,1:T(8,128)(2,1)} fusion(bf16[1024,768]{1,0:T(8,128)(2,1)S(1)} %get-tuple-element.44, bf16[1536,768]{1,0:T(8,128)(2,1)S(1)} %bitcast.64), kind=kOutput, calls=%fused_computation.4 | convolution fusion | flops 2419064832 | bytes 7077888 | tf_op jit(solution)/shard_map/dot_general | solution.py:150
  74.8 46.6 %reduce-scatter.2.cloned.1.call-done = bf16[1024,192]{0,1:T(8,128)(2,1)} async-done(((bf16[1024,1536]{0,1:T(8,128)(2,1)}), bf16[1024,192]{0,1:T(8,128)(2,1)}) %reduce-scatter.2.cloned.1.call-update) | async-done | bytes 393232 | tf_op jit(solution)/shard_map/reduce_scatter | solution.py:156
  122.5 2.0 fusion.20
  125.4 44.6 %all-gather.5.cloned.1.call-done = bf16[1024,1536]{0,1:T(8,128)(2,1)} async-done(((bf16[1024,192]{0,1:T(8,128)(2,1)}), bf16[1024,1536]{0,1:T(8,128)(2,1)}) %all-gather.5.cloned.1.call-update) | async-done | bytes 3145744 | tf_op jit(solution)/shard_map/all_gather | solution.py:168
  170.0 8.1 %multiply_convert_fusion.1 = bf16[1024,768]{1,0:T(8,128)(2,1)S(1)} fusion(f32[1024,768]{1,0:T(8,128)} %get-tuple-element.45, bf16[1024,1536]{0,1:T(8,128)(2,1)} %all-gather.5.cloned.1.call-done, bf16[1536,768]{1,0:T(8,128)(2,1)} %bitcast.63), kind=kOutput, calls=%fused_computation.9 | convolution fusion | flops 2432434176 | bytes 10223616 | tf_op jit(solution)/shard_map/dot_general | solution.py:170
  179.0 1.8 fusion.23
  180.8 1.8 fusion.21
  182.7 3.7 %fusion.7 = bf16[1536,384]{1,0:T(8,128)(2,1)S(1)} fusion(f32[1536,384]{1,0:T(8,128)S(1)} %fusion.23, bf16[1024,1536]{0,1:T(8,128)(2,1)} %collective-permute-done.1, bf16[1024,384]{1,0:T(8,128)(2,1)S(1)} %collective-permute-done.2), kind=kOutput, calls=%fused_computation.16 | convolution fusion | flops 1209729024 | bytes 7471104 | tf_op jit(solution)/shard_map/dot_general | solution.py:51
  186.4 3.7 %fusion.8 = bf16[1536,384]{1,0:T(8,128)(2,1)S(1)} fusion(f32[1536,384]{1,0:T(8,128)S(1)} %fusion.21, bf16[1024,1536]{0,1:T(8,128)(2,1)} %collective-permute-done.3, bf16[1024,384]{1,0:T(8,128)(2,1)S(1)} %collective-permute-done.4), kind=kOutput, calls=%fused_computation.17 | convolution fusion | flops 1209729024 | bytes 7471104 | tf_op jit(solution)/shard_map/dot_general | solution.py:51
  190.1 1.8 pad_maximum_fusion
  191.9 7.3 %all-to-all-start.1 = ((bf16[16,192,384]{2,1,0:T(8,128)(2,1)}), bf16[16,192,384]{2,1,0:T(8,128)(2,1)S(1)}, u32[]{:S(2)}, u32[]{:S(2)}) async-start(bf16[16,192,384]{2,1,0:T(8,128)(2,1)} %pad_maximum_fusion), calls=%async_computation.2 | async-start | bytes 4718592 | tf_op jit(solution)/shard_map/all_to_all | solution.py:184
  199.2 33.2 %all-to-all-done.1 = bf16[16,192,384]{2,1,0:T(8,128)(2,1)S(1)} async-done(((bf16[16,192,384]{2,1,0:T(8,128)(2,1)}), bf16[16,192,384]{2,1,0:T(8,128)(2,1)S(1)}, u32[]{:S(2)}, u32[]{:S(2)}) %all-to-all-start.1) | async-done | bytes 2359328 | tf_op jit(solution)/shard_map/all_to_all | solution.py:184
  233.5 1.3 compare_select_fusion
  235.6 11.7 %all-to-all-start.2 = ((f32[256,1,128]{2,1,0:T(1,128)}), f32[256,1,128]{2,1,0:T(1,128)S(1)}, u32[]{:S(2)}, u32[]{:S(2)}) async-start(f32[256,1,128]{2,1,0:T(1,128)} %iota.7), calls=%async_computation.3 | async-start | bytes 262144 | tf_op jit(solution)/shard_map/all_to_all | solution.py:57
  247.3 11.3 %all-to-all-done.2 = f32[256,1,128]{2,1,0:T(1,128)S(1)} async-done(((f32[256,1,128]{2,1,0:T(1,128)}), f32[256,1,128]{2,1,0:T(1,128)S(1)}, u32[]{:S(2)}, u32[]{:S(2)}) %all-to-all-start.2) | async-done | bytes 131104 | tf_op jit(solution)/shard_map/all_to_all | solution.py:57
  (67 shorter events, 11.3 us)
Async XLA Ops:
  7.2 4.8 %copy-start.4 = (f32[48,768]{1,0:T(8,128)S(1)}, f32[48,768]{1,0:T(8,128)}, u32[]{:S(2)}) copy-start(f32[48,768]{1,0:T(8,128)} %param.18) | copy-start | bytes 442372
  7.2 4.9 %copy-start.3 = (f32[48,768]{1,0:T(8,128)S(1)}, f32[48,768]{1,0:T(8,128)}, u32[]{:S(2)}) copy-start(f32[48,768]{1,0:T(8,128)} %param.19) | copy-start | bytes 442372
  7.2 52.9 %all-gather.3.cloned.1.call-start = ((), (), s32[]{:S(2)}) async-start(), calls=%async_computation.4 | async-start | bytes 3538944 | tf_op jit(solution)/shard_map/all_gather | solution.py:133
  12.0 109.4 %reduce-scatter.2.cloned.1.call-start = ((), (), s32[]{:S(2)}) async-start(), calls=%async_computation.5 | async-start | bytes 3538944 | tf_op jit(solution)/shard_map/reduce_scatter | solution.py:156
  49.4 4.7 %collective-permute-start = (bf16[16,96,768]{2,1,0:T(8,128)(2,1)S(1)}, bf16[16,96,768]{2,1,0:T(8,128)(2,1)}, u32[]{:S(2)}, u32[]{:S(2)}) collective-permute-start(bf16[16,96,768]{2,1,0:T(8,128)(2,1)S(1)} %all_to_all.16), channel_id=1, source_target_pairs={{0,8},{8,0},{1,9},{9,1},{2,10},{10,2},{3,11},{11,3},{4,12},{12,4},... | collective-permute-start | bytes 7077896 | tf_op jit(solution)/shard_map/ppermute | solution.py:22
  60.1 2.8 %copy-start = (bf16[1024,1536]{0,1:T(8,128)(2,1)S(1)}, bf16[1024,1536]{0,1:T(8,128)(2,1)}, u32[]{:S(2)}) copy-start(bf16[1024,1536]{0,1:T(8,128)(2,1)} %all-gather.3.cloned.1.call-done) | copy-start | bytes 9437188
  62.9 1.7 copy-start.2
  64.6 6.2 %copy-start.1 = (bf16[16,2,48,768]{3,2,1,0:T(8,128)(2,1)S(1)}, bf16[16,2,48,768]{3,2,1,0:T(8,128)(2,1)}, u32[]{:S(2)}) copy-start(bf16[16,2,48,768]{3,2,1,0:T(8,128)(2,1)} %copy.37) | copy-start | bytes 7077892
  69.6 1.2 copy-start.5
  74.8 95.2 %all-gather.5.cloned.1.call-start = ((), (), s32[]{:S(2)}) async-start(), calls=%async_computation.6 | async-start | bytes 3538944 | tf_op jit(solution)/shard_map/all_gather | solution.py:168
  125.3 57.3 %collective-permute-start.1 = (bf16[1024,1536]{0,1:T(8,128)(2,1)S(1)}, bf16[1024,1536]{0,1:T(8,128)(2,1)}, u32[]{:S(2)}, u32[]{:S(2)}) collective-permute-start(bf16[1024,1536]{0,1:T(8,128)(2,1)S(1)} %fusion.1), channel_id=1, source_target_pairs={{0,8},{8,0},{1,9},{9,1},{2,10},{10,2},{3,11},{11,3},{4,12},{12,4},... | collective-permute-start | bytes 9437192 | tf_op jit(solution)/shard_map/ppermute | solution.py:22
  170.0 16.4 %collective-permute-start.3 = (bf16[1024,1536]{0,1:T(8,128)(2,1)}, bf16[1024,1536]{0,1:T(8,128)(2,1)}, u32[]{:S(2)}, u32[]{:S(2)}) collective-permute-start(bf16[1024,1536]{0,1:T(8,128)(2,1)} %all-gather.5.cloned.1.call-done), channel_id=1, source_target_pairs={{0,8},{8,0},{1,9},{9,1},{2,10},{10,2},{3,11},{11,3},{4,12},{12,4},... | collective-permute-start | bytes 9437192 | tf_op jit(solution)/shard_map/ppermute | solution.py:22
  170.0 8.8 %copy-start.6 = (bf16[1024,768]{1,0:T(8,128)(2,1)S(1)}, bf16[1024,768]{1,0:T(8,128)(2,1)}, u32[]{:S(2)}) copy-start(bf16[1024,768]{1,0:T(8,128)(2,1)} %copy-done.5) | copy-start | bytes 4718596
  178.2 4.5 %collective-permute-start.2 = (bf16[1024,384]{1,0:T(8,128)(2,1)S(1)}, bf16[1024,384]{1,0:T(8,128)(2,1)S(1)}, u32[]{:S(2)}, u32[]{:S(2)}) collective-permute-start(bf16[1024,384]{1,0:T(8,128)(2,1)S(1)} %constant_dynamic-slice_fusion.1), channel_id=1, source_target_pairs={{0,8},{8,0},{1,9},{9,1},{2,10},{10,2},{3,11},{11,3},{4,12},{12,4},... | collective-permute-start | bytes 2359304 | tf_op jit(solution)/shard_map/ppermute | solution.py:22
  178.9 1.9 copy-start.11
  178.9 7.5 %collective-permute-start.4 = (bf16[1024,384]{1,0:T(8,128)(2,1)S(1)}, bf16[1024,384]{1,0:T(8,128)(2,1)S(1)}, u32[]{:S(2)}, u32[]{:S(2)}) collective-permute-start(bf16[1024,384]{1,0:T(8,128)(2,1)S(1)} %constant_dynamic-slice_fusion), channel_id=1, source_target_pairs={{0,8},{8,0},{1,9},{9,1},{2,10},{10,2},{3,11},{11,3},{4,12},{12,4},... | collective-permute-start | bytes 2359304 | tf_op jit(solution)/shard_map/ppermute | solution.py:22
  191.9 40.5 %all-to-all-start.1 = ((bf16[16,192,384]{2,1,0:T(8,128)(2,1)}), bf16[16,192,384]{2,1,0:T(8,128)(2,1)S(1)}, u32[]{:S(2)}, u32[]{:S(2)}) async-start(bf16[16,192,384]{2,1,0:T(8,128)(2,1)} %pad_maximum_fusion), calls=%async_computation.2 | async-start | bytes 4718592 | tf_op jit(solution)/shard_map/all_to_all | solution.py:184
  199.2 61.5 %copy-start.7 = (f32[48,768]{1,0:T(8,128)S(1)}, f32[48,768]{1,0:T(8,128)}, u32[]{:S(2)}) copy-start(f32[48,768]{1,0:T(8,128)} %param.21) | copy-start | bytes 442372
  199.2 61.5 %copy-start.8 = (f32[48,768]{1,0:T(8,128)S(1)}, f32[48,768]{1,0:T(8,128)}, u32[]{:S(2)}) copy-start(f32[48,768]{1,0:T(8,128)} %param.23) | copy-start | bytes 442372
  199.2 61.5 %copy-start.9 = (f32[48,768]{1,0:T(8,128)S(1)}, f32[48,768]{1,0:T(8,128)}, u32[]{:S(2)}) copy-start(f32[48,768]{1,0:T(8,128)} %param.22) | copy-start | bytes 442372
  199.2 61.5 %copy-start.10 = (f32[48,768]{1,0:T(8,128)S(1)}, f32[48,768]{1,0:T(8,128)}, u32[]{:S(2)}) copy-start(f32[48,768]{1,0:T(8,128)} %param.20) | copy-start | bytes 442372
  233.4 13.8 %collective-permute-start.5 = (f32[2,48,384]{2,1,0:T(8,128)S(1)}, f32[2,48,384]{2,1,0:T(8,128)S(1)}, u32[]{:S(2)}, u32[]{:S(2)}) collective-permute-start(f32[2,48,384]{2,1,0:T(8,128)S(1)} %get-tuple-element.35), channel_id=1, source_target_pairs={{0,8},{8,0},{1,9},{9,1},{2,10},{10,2},{3,11},{11,3},{4,12},{12,4},... | collective-permute-start | bytes 442376 | tf_op jit(solution)/shard_map/ppermute | solution.py:22
  235.6 23.1 %all-to-all-start.2 = ((f32[256,1,128]{2,1,0:T(1,128)}), f32[256,1,128]{2,1,0:T(1,128)S(1)}, u32[]{:S(2)}, u32[]{:S(2)}) async-start(f32[256,1,128]{2,1,0:T(1,128)} %iota.7), calls=%async_computation.3 | async-start | bytes 262144 | tf_op jit(solution)/shard_map/all_to_all | solution.py:57
Sparse Core Ops, SparseCore 0:
  12.1 47.9 all-gather.2
  74.9 46.4 reduce-scatter.1
  125.5 44.5 all-gather.4

commit v2 on v1

--- a/solution.py
+++ b/solution.py
@@ -1,10 +1,14 @@
+import functools
 import math
 
 import jax
 import jax.numpy as jnp
 from jax import lax
+from jax.experimental import pallas as pl
+from jax.experimental.pallas import tpu as pltpu
 from jax.sharding import Mesh
 from jax.sharding import PartitionSpec as P
+
 
 DP = ("y", "x", "c")
 DP_MP = ("y", "x", "c", "mp")
@@ -47,8 +51,100 @@
     return lax.dynamic_slice_in_dim(block, which * half, half, axis=1)
 
 
-def over_tokens(left, right):
-    return lax.dot_general(left, right, (((0,), (0,)), ((), ())), preferred_element_type=jnp.float32)
+def gradient_kernel(first, first_units, second, second_units, result, *, scale):
+    added = jnp.dot(first[...], first_units[...], preferred_element_type=jnp.float32)
+    added += jnp.dot(second[...], second_units[...], preferred_element_type=jnp.float32)
+    result[...] = (added * scale).astype(result.dtype)
+
+
+def weight_gradient(first, first_units, second, second_units, at, scale):
+    features, tokens = first.shape
+    units = first_units.shape[1]
+    block = features // 6
+    return pl.pallas_call(
+        functools.partial(gradient_kernel, scale=scale),
+        out_shape=jax.ShapeDtypeStruct((features, units), jnp.bfloat16),
+        grid=(features // block,),
+        in_specs=[
+            pl.BlockSpec((block, tokens), lambda i: (i, 0)),
+            pl.BlockSpec((tokens, units), lambda i: (0, 0)),
+            pl.BlockSpec((block, tokens), lambda i: (i + at[0], 0)),
+            pl.BlockSpec((tokens, units), lambda i: (0, at[1])),
+        ],
+        out_specs=pl.BlockSpec((block, units), lambda i: (i, 0)),
+        cost_estimate=pl.CostEstimate(
+            flops=4 * features * tokens * units,
+            transcendentals=0,
+            bytes_accessed=4 * (features + units) * tokens + 2 * features * units,
+        ),
+        compiler_params=pltpu.CompilerParams(dimension_semantics=("arbitrary",)),
+    )(first, first_units, second, second_units)
+
+
+def hidden_kernel(core, piece, down, slopes, mine, sent, *, scale):
+    summed = lax.dot_general(
+        piece[...], down[...], (((0,), (0,)), ((), ())), preferred_element_type=jnp.float32
+    )
+    rounded = (summed * scale * slopes[...]).astype(mine.dtype)
+    half = mine.shape[1]
+    low, high = rounded[:, :half], rounded[:, half:]
+
+    @pl.when(core[0] == 0)
+    def _():
+        mine[...] = low
+        sent[...] = high
+
+    @pl.when(core[0] != 0)
+    def _():
+        mine[...] = high
+        sent[...] = low
+
+
+def hidden_gradient(core, piece, down, slopes, scale):
+    features, tokens = piece.shape
+    units = down.shape[1]
+    block = tokens // 4
+    half = jax.ShapeDtypeStruct((tokens, units // 2), jnp.bfloat16)
+    return pl.pallas_call(
+        functools.partial(hidden_kernel, scale=scale),
+        out_shape=(half, half),
+        grid=(tokens // block,),
+        in_specs=[
+            pl.BlockSpec(memory_space=pltpu.SMEM),
+            pl.BlockSpec((features, block), lambda i: (0, i)),
+            pl.BlockSpec((features, units), lambda i: (0, 0)),
+            pl.BlockSpec((block, units), lambda i: (i, 0)),
+        ],
+        out_specs=(
+            pl.BlockSpec((block, units // 2), lambda i: (i, 0)),
+            pl.BlockSpec((block, units // 2), lambda i: (i, 0)),
+        ),
+        cost_estimate=pl.CostEstimate(
+            flops=2 * features * tokens * units,
+            transcendentals=0,
+            bytes_accessed=2 * features * (tokens + units) + 6 * tokens * units,
+        ),
+        compiler_params=pltpu.CompilerParams(dimension_semantics=("arbitrary",)),
+        name="hidden_gradient",
+    )(core.reshape(1), piece, down, slopes)
+
+
+def from_plane(halves):
+    parts = lax.all_to_all(halves, PLANE, split_axis=0, concat_axis=0, tiled=True)
+    return jnp.sum(parts.astype(jnp.float32), axis=0)
+
+
+def from_axis(blocks, axis):
+    size = lax.axis_size(axis)
+    here = lax.axis_index(axis)
+    total = lax.dynamic_index_in_dim(blocks, here, 0, keepdims=False).astype(jnp.float32)
+    for step in range(1, size):
+        sent = lax.dynamic_index_in_dim(blocks, (here + step) % size, 0, keepdims=False)
+        moved = lax.ppermute(
+            sent.astype(jnp.bfloat16), axis, [(i, (i + step) % size) for i in range(size)]
+        )
+        total = total + moved.astype(jnp.float32)
+    return total
 
 
 def totals(first, second):
@@ -59,6 +155,10 @@
     )
     summed = jnp.sum(rows, axis=0)
     return summed[0], summed[64]
+
+
+def over_features(left, right):
+    return lax.dot_general(left, right, (((0,), (0,)), ((), ())), preferred_element_type=jnp.float32)
 
 
 def gelu_pair(preact):
@@ -71,30 +171,29 @@
     return (activation, slopes)
 
 
-def distill_target(clean, noise, teacher_first, teacher_second, step_index, teacher_count):
-    steps_float = teacher_count.astype(jnp.float32)[:, None, None]
-    doubled = 2.0 * step_index.astype(jnp.float32)[:, None, None]
-    quarter_turn = 0.5 * math.pi
-    time_now = doubled / steps_float
-    time_mid = (doubled - 1.0) / steps_float
-    time_end = (doubled - 2.0) / steps_float
-    alpha_now = jnp.cos(quarter_turn * time_now)
-    sigma_now = jnp.sin(quarter_turn * time_now)
-    alpha_mid = jnp.cos(quarter_turn * time_mid)
-    sigma_mid = jnp.sin(quarter_turn * time_mid)
-    alpha_end = jnp.cos(quarter_turn * time_end)
-    sigma_end = jnp.sin(quarter_turn * time_end)
+def rates(step_index, teacher_count):
+    steps_float = teacher_count.astype(jnp.float32)
+    doubled = 2.0 * step_index.astype(jnp.float32)
+    back = jnp.arange(3, dtype=jnp.float32)[:, None]
+    angles = 0.5 * math.pi * ((doubled - back) / steps_float)
+    return jnp.cos(angles)[:, :, None, None], jnp.sin(angles)[:, :, None, None]
+
+
+def noisy_latent(clean, noise, alphas, sigmas):
+    return alphas[0] * clean.astype(jnp.float32) + sigmas[0] * noise.astype(jnp.float32)
+
+
+def distill_target(latent_now, teacher_first, teacher_second, alphas, sigmas):
+    alpha_now, alpha_mid, alpha_end = alphas
+    sigma_now, sigma_mid, sigma_end = sigmas
     first_f = teacher_first.astype(jnp.float32)
     second_f = teacher_second.astype(jnp.float32)
-    latent_now = alpha_now * clean.astype(jnp.float32) + sigma_now * noise.astype(jnp.float32)
     noise_now = (latent_now - alpha_now * first_f) / sigma_now
     latent_mid = alpha_mid * first_f + sigma_mid * noise_now
     noise_mid = (latent_mid - alpha_mid * second_f) / sigma_mid
     latent_end = alpha_end * second_f + sigma_end * noise_mid
     sigma_ratio = sigma_end / sigma_now
-    target = (latent_end - sigma_ratio * latent_now) / (alpha_end - sigma_ratio * alpha_now)
-    weighting = jnp.maximum(alpha_now * alpha_now / (sigma_now * sigma_now), 1.0)[:, 0, 0]
-    return (latent_now, target, weighting)
+    return (latent_end - sigma_ratio * latent_now) / (alpha_end - sigma_ratio * alpha_now)
 
 
 def adam_update(master, moment, second, gradient, factor):
@@ -126,14 +225,20 @@
     samples_dev, token_count, width_local = clean.shape
     sample_total = samples_dev * lax.axis_size(DP)
     row_count = samples_dev * token_count
-    latent, target, weighting = distill_target(
-        clean, noise, teacher_first, teacher_second, step_index, teacher_count
-    )
+    alphas, sigmas = rates(step_index, teacher_count)
+    weighting = jnp.maximum(alphas[0] * alphas[0] / (sigmas[0] * sigmas[0]), 1.0)
+    latent = noisy_latent(clean, noise, alphas, sigmas)
     noisy_rows = latent.reshape(row_count, width_local).astype(jnp.bfloat16)
-    gathered = lax.all_gather(noisy_rows, "mp", axis=1, tiled=True)
+    gathered = lax.all_gather(noisy_rows.T, "mp", axis=0, tiled=True)
+    *held, gathered = lax.optimization_barrier(
+        (clean, noise, teacher_first, teacher_second, gathered)
+    )
+    latent_again = noisy_latent(*held[:2], alphas, sigmas)
+    target = distill_target(latent_again, *held[2:], alphas, sigmas)
+    offset = latent_again - target
     gathered_f = gathered.astype(jnp.float32)
     normed = (
-        gathered_f * lax.rsqrt(jnp.mean(gathered_f * gathered_f, axis=1, keepdims=True) + 1e-06)
+        gathered_f * lax.rsqrt(jnp.mean(gathered_f * gathered_f, axis=0, keepdims=True) + 1e-06)
     ).astype(jnp.bfloat16)
     up_full, down_full = gathered_weights(
         up_master.astype(jnp.bfloat16), down_master.astype(jnp.bfloat16)
@@ -142,49 +247,49 @@
     hidden_local = up_full.shape[1]
     dscale = width_full ** (-0.5)
     fscale = (hidden_local * lax.axis_size("mp")) ** (-0.5)
-    preact = jnp.dot(normed, up_full, preferred_element_type=jnp.float32) * dscale
+    preact = over_features(normed, up_full) * dscale
     activation, slopes = gelu_pair(preact)
     hidden = activation.astype(jnp.bfloat16)
     core = lax.axis_index("c")
     partial_value = (
         lax.dot_general(
-            hidden, down_full, (((1,), (1,)), ((), ())), preferred_element_type=jnp.float32
+            down_full, hidden, (((1,), (1,)), ((), ())), preferred_element_type=jnp.float32
         )
         * fscale
     ).astype(jnp.bfloat16)
-    offset = lax.optimization_barrier(latent - target)
-    branch = lax.psum_scatter(partial_value, "mp", scatter_dimension=1, tiled=True).astype(
+    branch = lax.psum_scatter(partial_value, "mp", scatter_dimension=0, tiled=True).astype(
         jnp.float32
     )
-    normed_other, hidden_other = core_swapped(normed), core_swapped(half_columns(hidden, 1 - core))
-    errors = offset + branch.reshape(latent.shape)
-    weight_cube = weighting[:, None, None]
+    offset, normed_other, hidden_mine, hidden_other = lax.optimization_barrier(
+        (
+            offset,
+            core_swapped(normed),
+            half_columns(hidden, core),
+            core_swapped(half_columns(hidden, 1 - core)),
+        )
+    )
+    errors = offset + branch.T.reshape(latent.shape)
+    weight_cube = weighting
     loss_part = jnp.sum(weight_cube * errors * errors)
     dpred = (
         (2.0 * weight_cube / sample_total * errors)
         .astype(jnp.bfloat16)
         .reshape(row_count, width_local)
     )
-    piece = lax.all_gather(dpred, "mp", axis=1, tiled=True)
+    piece = lax.all_gather(dpred.T, "mp", axis=0, tiled=True)
     piece_other = core_swapped(piece)
-    summed = jnp.dot(piece, down_full, preferred_element_type=jnp.float32)
-    dpre = (summed * fscale * slopes).astype(jnp.bfloat16)
-    dpre_other = core_swapped(half_columns(dpre, 1 - core))
-    grad_down = (
-        over_tokens(piece, half_columns(hidden, core)) + over_tokens(piece_other, hidden_other)
-    ) * fscale
-    grad_up = (
-        over_tokens(normed, half_columns(dpre, core)) + over_tokens(normed_other, dpre_other)
-    ) * dscale
+    dpre_mine, dpre_sent = hidden_gradient(core, piece, down_full, slopes, fscale)
+    dpre_other = core_swapped(dpre_sent)
+    grad_down = weight_gradient(piece, hidden_mine, piece_other, hidden_other, (0, 0), fscale)
+    grad_up = weight_gradient(normed, dpre_mine, normed_other, dpre_other, (0, 0), dscale)
     chips = lax.axis_size(PLANE)
     rows_chip = width_full // chips
-    halves = [
-        g.astype(jnp.bfloat16).reshape(chips, rows_chip, -1) for g in (grad_up, grad_down)
-    ]
-    parts = lax.all_to_all(
-        jnp.concatenate(halves, axis=1), PLANE, split_axis=0, concat_axis=0, tiled=True
-    )
-    chip_rows = jnp.sum(parts.astype(jnp.float32), axis=0)
+    rows_down = from_plane(grad_down.reshape(chips, rows_chip, -1))
+    blocks_up = grad_up.reshape(
+        lax.axis_size("y"), lax.axis_size("x"), rows_chip, -1
+    )
+    rows_up = from_axis(from_axis(jnp.swapaxes(blocks_up, 0, 1), "x"), "y")
+    chip_rows = jnp.stack([rows_up, rows_down])
     squares = jnp.sum(chip_rows * chip_rows)
     loss_total, square_total = totals(loss_part, squares)
     by_core = chip_rows.reshape(2, 2, rows_chip // 2, -1)

time: 272 us -> 282 us (1.037)
  Pallas kernels: 0 us -> 23.2 us
  matrix products: 28.1 us -> 10.1 us
  waiting for transfers between devices: 141 us -> 132 us
  starting transfers between devices: 20 us -> 26.3 us
  local copies, waits for them, and re-layouts: 9.1 us -> 14.6 us
    all_to_all x1, waiting for transfers between devices: 33.2 us -> 0.01 us  [from_plane(): lax.all_to_all(halves, PLANE, split_axis=0, concat_axis=0, tiled=True)]
    ppermute x0 -> x6, waiting for transfers between devices: none -> 29 us  [from_axis(): lax.ppermute(sent.astype(jnp.bfloat16), axis, [(i, (i + step) % size) for...]
    pallas_call x0 -> x3, Pallas kernels: none -> 23.2 us  [the longest x2 16 us: weight_gradient(): pl.pallas_call(functools.partial(gradient_kernel, scale=scale), out_shape...]
    dot_general x7 -> x2, matrix products: 28.1 us -> 10.1 us  [the longest x1 6.1 us: over_features(): lax.dot_general(left, right, (((0,), (0,)), ((), ())), preferred_element_...]
    ppermute x0 -> x6, starting transfers between devices: none -> 9.02 us  [from_axis(): lax.ppermute(sent.astype(jnp.bfloat16), axis, [(i, (i + step) % size) for...]
    reduce_scatter x1, waiting for transfers between devices: 46.6 us -> 38.9 us  [per_device(): lax.psum_scatter(partial_value, 'mp', scatter_dimension=0, tiled=True)]
    ppermute x6, waiting for transfers between devices: 4.51 us -> 7.69 us  [core_swapped(): return lax.ppermute(block, 'c', [(0, 1), (1, 0)])]
    all_to_all x1, starting transfers between devices: 11.7 us -> 8.63 us  [totals(): lax.all_to_all(jnp.where(lane < 64, first, second), DP_MP, split_axis=0,...]
  transfers between devices with their start and end apart: 11 -> 17, of which waited for: 6 -> 12; matrix products, arithmetic and copies ran while one was open for 9% -> 5% of each run, Pallas kernels for 0% -> 5%
where the time goes in v2:
time: 282 us; the launch traced here: 279 us
  waiting for transfers between devices  132 us (47%)
  blocking collectives  37.1 us (13%)
  starting transfers between devices  26.3 us (9%)
  Pallas kernels  23.2 us (8%)
  other arithmetic  18.9 us (7%)
  between operations  16.7 us (6%)
  local copies, waits for them, and re-layouts  14.6 us (5%)
  matrix products  10.1 us (4%)
    all_gather x1, waiting for transfers between devices, per_device(): piece = lax.all_gather(dpred.T, 'mp', axis=0, tiled=True)  44.5 us
    reduce_scatter x1, waiting for transfers between devices, per_device(): lax.psum_scatter(partial_value, 'mp', scatter_dimension=0, tiled=True)  38.9 us
    all_to_all x1, blocking collectives, gathered_weights(): lax.all_to_all(jnp.broadcast_to(both, (chips,) + both.shape), PLANE, spli...  37.1 us
    ppermute x6, waiting for transfers between devices, from_axis(): lax.ppermute(sent.astype(jnp.bfloat16), axis, [(i, (i + step) % size) for...  29 us
    pallas_call x2, Pallas kernels, weight_gradient(): pl.pallas_call(functools.partial(gradient_kernel, scale=scale), out_shape...  16 us
    all_to_all x1, waiting for transfers between devices, totals(): lax.all_to_all(jnp.where(lane < 64, first, second), DP_MP, split_axis=0,...  11.3 us
    ppermute x6, starting transfers between devices, from_axis(): lax.ppermute(sent.astype(jnp.bfloat16), axis, [(i, (i + step) % size) for...  9.02 us
    all_to_all x1, starting transfers between devices, totals(): lax.all_to_all(jnp.where(lane < 64, first, second), DP_MP, split_axis=0,...  8.63 us
  transfers between devices with their start and end apart: 17, of which 12 were waited for; matrix products, arithmetic and copies ran while one was open for 5% of the time, Pallas kernels for 5%

profile of v2, /device:TPU:2, one launch (start us, length us, event | category | flops | bytes accessed | tf_op | source)
XLA Modules:
  0.0 278.7 jit_solution(16899577854693398934)
XLA Ops:
  11.7 37.1 %all_to_all.16 = bf16[16,96,768]{2,1,0:T(8,128)(2,1)S(1)} all-to-all(bf16[16,96,768]{2,1,0:T(8,128)(2,1)S(1)} %broadcast_in_dim.8), channel_id=1, replica_groups=mesh['y'=4,'x'=4,'c'=2,'mp'=8] {'y','x'}, dimensions={0} | all-to-all | bytes 4718592 | tf_op jit(solution)/shard_map/all_to_all | solution.py:39
  49.0 4.5 %collective-permute-done.1 = bf16[16,96,768]{2,1,0:T(8,128)(2,1)} collective-permute-done((bf16[16,96,768]{2,1,0:T(8,128)(2,1)S(1)}, bf16[16,96,768]{2,1,0:T(8,128)(2,1)}, u32[]{:S(2)}, u32[]{:S(2)}) %collective-permute-start.1) | collective-permute-done | bytes 2359328 | tf_op jit(solution)/shard_map/ppermute | solution.py:26
  53.5 1.8 slice_bitcast_fusion
  57.4 1.6 maximum_select_fusion
  59.5 2.7 fusion
  64.0 6.1 %multiply_add_fusion.1 = (f32[1024,768]{1,0:T(8,128)}, bf16[1024,768]{1,0:T(8,128)(2,1)S(1)}) fusion(bf16[1536,1024]{1,0:T(8,128)(2,1)S(1)} %fusion.1.first, bf16[1536,768]{1,0:T(8,128)(2,1)S(1)} %bitcast.121), kind=kOutput, calls=%fused_computation.8 | convolution fusion | flops 2431647744 | bytes 10223616 | tf_op jit(solution)/shard_map/dot_general | solution.py:161
  71.2 4.0 %multiply_convert_fusion = bf16[1536,1024]{1,0:T(8,128)(2,1)} fusion(bf16[1536,768]{1,0:T(8,128)(2,1)S(1)} %bitcast.120, bf16[1024,768]{1,0:T(8,128)(2,1)S(1)} %get-tuple-element.40), kind=kOutput, calls=%fused_computation.4 | convolution fusion | flops 2419064832 | bytes 7077888 | tf_op jit(solution)/shard_map/dot_general | solution.py:255
  75.5 2.5 constant_dynamic-slice_fusion
  79.0 2.3 fusion.8
  83.1 38.9 %reduce-scatter.2.cloned.1.call-done = bf16[192,1024]{1,0:T(8,128)(2,1)} async-done(((bf16[1536,1024]{1,0:T(8,128)(2,1)}), bf16[192,1024]{1,0:T(8,128)(2,1)}) %reduce-scatter.2.cloned.1.call-update) | async-done | bytes 393232 | tf_op jit(solution)/shard_map/reduce_scatter | solution.py:260
  123.1 2.0 fusion.16
  126.0 44.5 %all-gather.5.cloned.1.call-done.piece.first = bf16[1536,1024]{1,0:T(8,128)(2,1)} async-done(((bf16[192,1024]{1,0:T(8,128)(2,1)}), bf16[1536,1024]{1,0:T(8,128)(2,1)}) %all-gather.5.cloned.1.call-update) | async-done | bytes 3145744 | tf_op jit(solution)/shard_map/all_gather | solution.py:279
  170.5 7.2 %hidden_gradient.1 = (bf16[1024,384]{1,0:T(8,128)(2,1)}, bf16[1024,384]{1,0:T(8,128)(2,1)}) custom-call(s32[1]{0:T(128)} %bitcast.3.core, bf16[1536,1024]{1,0:T(8,128)(2,1)} %all-gather.5.cloned.1.call-done.piece.first, bf16[1536,768]{1,0:T(8,128)(2,1)} %bitcast.119, f32[1024,768]{1,0:T(8,128)} %get-tuple-element.39.slopes), custom_call_target="tpu_custom_call" | custom-call | flops 2415919104 | bytes 10223616 | tf_op jit(solution)/shard_map/hidden_gradient/pallas_call | solution.py:108
  178.2 2.3 collective-permute-done.3.second_units
  180.4 8.0 %shard_map.171 = bf16[1536,384]{1,0:T(8,128)(2,1)} custom-call(bf16[1536,1024]{1,0:T(8,128)(2,1)} %copy-done, bf16[1024,384]{1,0:T(8,128)(2,1)} %get-tuple-element.24.first_units, bf16[1536,1024]{1,0:T(8,128)(2,1)} %collective-permute-done.second, bf16[1024,384]{1,0:T(8,128)(2,1)} %collective-permute-done.3.second_units), custom_call_target="tpu_custom_call" | custom-call | flops 2415919104 | bytes 9043968 | tf_op jit(solution)/shard_map/pallas_call | solution.py:64
  188.4 1.6 copy-done.3
  190.1 8.0 %shard_map.172 = bf16[1536,384]{1,0:T(8,128)(2,1)} custom-call(bf16[1536,1024]{1,0:T(8,128)(2,1)} %all-gather.5.cloned.1.call-done.piece.first, bf16[1024,384]{1,0:T(8,128)(2,1)} %get-tuple-element.27.first_units, bf16[1536,1024]{1,0:T(8,128)(2,1)} %copy-done.3, bf16[1024,384]{1,0:T(8,128)(2,1)} %copy-done.9), custom_call_target="tpu_custom_call" | custom-call | flops 2415919104 | bytes 9043968 | tf_op jit(solution)/shard_map/pallas_call | solution.py:64
  198.1 7.4 %all-to-all-start.1 = ((bf16[16,96,384]{2,1,0:T(8,128)(2,1)}), bf16[16,96,384]{2,1,0:T(8,128)(2,1)S(1)}, u32[]{:S(2)}, u32[]{:S(2)}) async-start(bf16[16,96,384]{2,1,0:T(8,128)(2,1)} %bitcast.117), calls=%async_computation.2 | async-start | bytes 2359296 | tf_op jit(solution)/shard_map/all_to_all | solution.py:133
  207.7 2.1 collective-permute-start.5
  209.8 23.4 %collective-permute-done.4 = bf16[4,96,384]{2,1,0:T(8,128)(2,1)S(1)} collective-permute-done((bf16[4,96,384]{2,1,0:T(8,128)(2,1)S(1)}, bf16[4,96,384]{2,1,0:T(8,128)(2,1)S(1)}, u32[]{:S(2)}, u32[]{:S(2)}) %collective-permute-start.4) | collective-permute-done | bytes 294944 | tf_op jit(solution)/shard_map/ppermute | solution.py:143
  236.7 2.3 collective-permute-start.9
  241.6 3.3 %collective-permute-done.8 = bf16[96,384]{1,0:T(8,128)(2,1)S(1)} collective-permute-done((bf16[96,384]{1,0:T(8,128)(2,1)S(1)}, bf16[96,384]{1,0:T(8,128)(2,1)S(1)}, u32[]{:S(2)}, u32[]{:S(2)}) %collective-permute-start.8) | collective-permute-done | bytes 73760 | tf_op jit(solution)/shard_map/ppermute | solution.py:143
  247.9 8.6 %all-to-all-start.2 = ((f32[256,1,128]{2,1,0:T(1,128)}), f32[256,1,128]{2,1,0:T(1,128)S(1)}, u32[]{:S(2)}, u32[]{:S(2)}) async-start(f32[256,1,128]{2,1,0:T(1,128)} %iota.11), calls=%async_computation.3 | async-start | bytes 262144 | tf_op jit(solution)/shard_map/all_to_all | solution.py:153
  256.6 11.3 %all-to-all-done.2 = f32[256,1,128]{2,1,0:T(1,128)S(1)} async-done(((f32[256,1,128]{2,1,0:T(1,128)}), f32[256,1,128]{2,1,0:T(1,128)S(1)}, u32[]{:S(2)}, u32[]{:S(2)}) %all-to-all-start.2) | async-done | bytes 131104 | tf_op jit(solution)/shard_map/all_to_all | solution.py:153
  (100 shorter events, 28.5 us)
Async XLA Ops:
  7.2 52.3 %all-gather.3.cloned.1.call-start = ((), (), s32[]{:S(2)}) async-start(), calls=%async_computation.4 | async-start | bytes 3538944 | tf_op jit(solution)/shard_map/all_gather | solution.py:232
  11.4 110.6 %reduce-scatter.2.cloned.1.call-start = ((), (), s32[]{:S(2)}) async-start(), calls=%async_computation.5 | async-start | bytes 3538944 | tf_op jit(solution)/shard_map/reduce_scatter | solution.py:260
  48.8 4.7 %collective-permute-start.1 = (bf16[16,96,768]{2,1,0:T(8,128)(2,1)S(1)}, bf16[16,96,768]{2,1,0:T(8,128)(2,1)}, u32[]{:S(2)}, u32[]{:S(2)}) collective-permute-start(bf16[16,96,768]{2,1,0:T(8,128)(2,1)S(1)} %all_to_all.16), channel_id=1, source_target_pairs={{0,8},{8,0},{1,9},{9,1},{2,10},{10,2},{3,11},{11,3},{4,12},{12,4},... | collective-permute-start | bytes 7077896 | tf_op jit(solution)/shard_map/ppermute | solution.py:26
  75.3 95.2 %all-gather.5.cloned.1.call-start = ((), (), s32[]{:S(2)}) async-start(), calls=%async_computation.6 | async-start | bytes 3538944 | tf_op jit(solution)/shard_map/all_gather | solution.py:279
  75.4 6.9 %collective-permute-start = (bf16[1536,1024]{1,0:T(8,128)(2,1)S(1)}, bf16[1536,1024]{1,0:T(8,128)(2,1)}, u32[]{:S(2)}, u32[]{:S(2)}) collective-permute-start(bf16[1536,1024]{1,0:T(8,128)(2,1)S(1)} %fusion.1.first), channel_id=1, source_target_pairs={{0,8},{8,0},{1,9},{9,1},{2,10},{10,2},{3,11},{11,3},{4,12},{12,4},... | collective-permute-start | bytes 9437192 | tf_op jit(solution)/shard_map/ppermute | solution.py:26
  78.0 4.2 %collective-permute-start.2 = (bf16[1024,384]{1,0:T(8,128)(2,1)S(1)}, bf16[1024,384]{1,0:T(8,128)(2,1)S(1)}, u32[]{:S(2)}, u32[]{:S(2)}) collective-permute-start(bf16[1024,384]{1,0:T(8,128)(2,1)S(1)} %get-tuple-element.47), channel_id=1, source_target_pairs={{0,8},{8,0},{1,9},{9,1},{2,10},{10,2},{3,11},{11,3},{4,12},{12,4},... | collective-permute-start | bytes 2359304 | tf_op jit(solution)/shard_map/ppermute | solution.py:26
  79.0 44.1 %copy-start.20 = (f32[4]{0:T(128)S(1)}, f32[4]{0:T(128)}, u32[]{:S(2)}) copy-start(f32[4]{0:T(128)} %get-tuple-element.60) | copy-start | bytes 52
  79.0 44.1 %copy-start.21 = (f32[4]{0:T(128)S(1)}, f32[4]{0:T(128)}, u32[]{:S(2)}) copy-start(f32[4]{0:T(128)} %get-tuple-element.61) | copy-start | bytes 52
  170.5 17.9 %collective-permute-start.10 = (bf16[1536,1024]{1,0:T(8,128)(2,1)}, bf16[1536,1024]{1,0:T(8,128)(2,1)S(1)}, u32[]{:S(2)}, u32[]{:S(2)}) collective-permute-start(bf16[1536,1024]{1,0:T(8,128)(2,1)} %all-gather.5.cloned.1.call-done.piece.first), channel_id=1, source_target_pairs={{0,8},{8,0},{1,9},{9,1},{2,10},{10,2},{3,11},{11,3},{4,12},{12,4},... | collective-permute-start | bytes 9437192 | tf_op jit(solution)/shard_map/ppermute | solution.py:26
  177.7 2.7 collective-permute-start.3
  198.1 46.9 %all-to-all-start.1 = ((bf16[16,96,384]{2,1,0:T(8,128)(2,1)}), bf16[16,96,384]{2,1,0:T(8,128)(2,1)S(1)}, u32[]{:S(2)}, u32[]{:S(2)}) async-start(bf16[16,96,384]{2,1,0:T(8,128)(2,1)} %bitcast.117), calls=%async_computation.2 | async-start | bytes 2359296 | tf_op jit(solution)/shard_map/all_to_all | solution.py:133
  205.6 27.5 %collective-permute-start.4 = (bf16[4,96,384]{2,1,0:T(8,128)(2,1)S(1)}, bf16[4,96,384]{2,1,0:T(8,128)(2,1)S(1)}, u32[]{:S(2)}, u32[]{:S(2)}) collective-permute-start(bf16[4,96,384]{2,1,0:T(8,128)(2,1)S(1)} %get-tuple-element.49), channel_id=1, source_target_pairs={{0,16},{16,32},{32,48},{48,0},{1,17},{17,33},{33,49},{49,1},{2,18}... | collective-permute-start | bytes 884744 | tf_op jit(solution)/shard_map/ppermute | solution.py:143
  207.1 26.0 %collective-permute-start.6 = (bf16[4,96,384]{2,1,0:T(8,128)(2,1)S(1)}, bf16[4,96,384]{2,1,0:T(8,128)(2,1)}, u32[]{:S(2)}, u32[]{:S(2)}) collective-permute-start(bf16[4,96,384]{2,1,0:T(8,128)(2,1)S(1)} %get-tuple-element.50), channel_id=1, source_target_pairs={{0,48},{16,0},{32,16},{48,32},{1,49},{17,1},{33,17},{49,33},{2,50}... | collective-permute-start | bytes 884744 | tf_op jit(solution)/shard_map/ppermute | solution.py:143
  207.7 26.7 %collective-permute-start.5 = (bf16[4,96,384]{2,1,0:T(8,128)(2,1)S(1)}, bf16[4,96,384]{2,1,0:T(8,128)(2,1)}, u32[]{:S(2)}, u32[]{:S(2)}) collective-permute-start(bf16[4,96,384]{2,1,0:T(8,128)(2,1)S(1)} %get-tuple-element.51), channel_id=1, source_target_pairs={{0,32},{16,48},{32,0},{48,16},{1,33},{17,49},{33,1},{49,17},{2,34}... | collective-permute-start | bytes 884744 | tf_op jit(solution)/shard_map/ppermute | solution.py:143
  235.6 34.4 %copy-start.11 = (f32[48,768]{1,0:T(8,128)S(1)}, f32[48,768]{1,0:T(8,128)}, u32[]{:S(2)}) copy-start(f32[48,768]{1,0:T(8,128)} %param.19) | copy-start | bytes 442372
  235.6 34.4 %copy-start.13 = (f32[48,768]{1,0:T(8,128)S(1)}, f32[48,768]{1,0:T(8,128)}, u32[]{:S(2)}) copy-start(f32[48,768]{1,0:T(8,128)} %param.18) | copy-start | bytes 442372
  235.6 34.4 %copy-start.16 = (f32[48,768]{1,0:T(8,128)S(1)}, f32[48,768]{1,0:T(8,128)}, u32[]{:S(2)}) copy-start(f32[48,768]{1,0:T(8,128)} %param.21) | copy-start | bytes 442372
  235.6 34.4 %copy-start.17 = (f32[48,768]{1,0:T(8,128)S(1)}, f32[48,768]{1,0:T(8,128)}, u32[]{:S(2)}) copy-start(f32[48,768]{1,0:T(8,128)} %param.23) | copy-start | bytes 442372
  235.6 34.4 %copy-start.18 = (f32[48,768]{1,0:T(8,128)S(1)}, f32[48,768]{1,0:T(8,128)}, u32[]{:S(2)}) copy-start(f32[48,768]{1,0:T(8,128)} %param.22) | copy-start | bytes 442372
  235.7 5.6 %collective-permute-start.7 = (bf16[96,384]{1,0:T(8,128)(2,1)S(1)}, bf16[96,384]{1,0:T(8,128)(2,1)S(1)}, u32[]{:S(2)}, u32[]{:S(2)}) collective-permute-start(bf16[96,384]{1,0:T(8,128)(2,1)S(1)} %get-tuple-element.52), channel_id=1, source_target_pairs={{0,64},{64,128},{128,192},{192,0},{1,65},{65,129},{129,193},{193,1... | collective-permute-start | bytes 221192 | tf_op jit(solution)/shard_map/ppermute | solution.py:143
  236.7 4.9 %collective-permute-start.9 = (bf16[96,384]{1,0:T(8,128)(2,1)S(1)}, bf16[96,384]{1,0:T(8,128)(2,1)S(1)}, u32[]{:S(2)}, u32[]{:S(2)}) collective-permute-start(bf16[96,384]{1,0:T(8,128)(2,1)S(1)} %get-tuple-element.53), channel_id=1, source_target_pairs={{0,192},{64,0},{128,64},{192,128},{1,193},{65,1},{129,65},{193,129... | collective-permute-start | bytes 221192 | tf_op jit(solution)/shard_map/ppermute | solution.py:143
  239.0 5.9 %collective-permute-start.8 = (bf16[96,384]{1,0:T(8,128)(2,1)S(1)}, bf16[96,384]{1,0:T(8,128)(2,1)S(1)}, u32[]{:S(2)}, u32[]{:S(2)}) collective-permute-start(bf16[96,384]{1,0:T(8,128)(2,1)S(1)} %get-tuple-element.54), channel_id=1, source_target_pairs={{0,128},{64,192},{128,0},{192,64},{1,129},{65,193},{129,1},{193,65... | collective-permute-start | bytes 221192 | tf_op jit(solution)/shard_map/ppermute | solution.py:143
  245.1 11.4 %collective-permute-start.11 = (f32[2,48,384]{2,1,0:T(8,128)S(1)}, f32[2,48,384]{2,1,0:T(8,128)S(1)}, u32[]{:S(2)}, u32[]{:S(2)}) collective-permute-start(f32[2,48,384]{2,1,0:T(8,128)S(1)} %get-tuple-element.59), channel_id=1, source_target_pairs={{0,8},{8,0},{1,9},{9,1},{2,10},{10,2},{3,11},{11,3},{4,12},{12,4},... | collective-permute-start | bytes 442376 | tf_op jit(solution)/shard_map/ppermute | solution.py:26
  247.9 20.0 %all-to-all-start.2 = ((f32[256,1,128]{2,1,0:T(1,128)}), f32[256,1,128]{2,1,0:T(1,128)S(1)}, u32[]{:S(2)}, u32[]{:S(2)}) async-start(f32[256,1,128]{2,1,0:T(1,128)} %iota.11), calls=%async_computation.3 | async-start | bytes 262144 | tf_op jit(solution)/shard_map/all_to_all | solution.py:153
  (15 other events, 92.2 us)
Sparse Core Ops, SparseCore 0:
  11.5 47.9 all-gather.2
  75.4 46.5 reduce-scatter.1
  126.1 44.3 all-gather.4

commit v3 on v2

--- a/solution.py
+++ b/solution.py
@@ -46,39 +46,69 @@
     )
 
 
-def half_columns(block, which):
-    half = block.shape[1] // 2
-    return lax.dynamic_slice_in_dim(block, which * half, half, axis=1)
-
-
-def gradient_kernel(first, first_units, second, second_units, result, *, scale):
-    added = jnp.dot(first[...], first_units[...], preferred_element_type=jnp.float32)
-    added += jnp.dot(second[...], second_units[...], preferred_element_type=jnp.float32)
-    result[...] = (added * scale).astype(result.dtype)
-
-
-def weight_gradient(first, first_units, second, second_units, at, scale):
-    features, tokens = first.shape
-    units = first_units.shape[1]
-    block = features // 6
+def halves_kept(core, block, mine, sent):
+    half = mine.shape[1]
+
+    @pl.when(core == 0)
+    def _():
+        mine[...] = block[:, :half]
+        sent[...] = block[:, half:]
+
+    @pl.when(core != 0)
+    def _():
+        mine[...] = block[:, half:]
+        sent[...] = block[:, :half]
+
+
+def forward_kernel(core, gathered, up, down, normed, mine, sent, slopes, partial, *, up_scale, down_scale):
+    tokens = gathered[...].astype(jnp.float32)
+    mean = jnp.mean(tokens * tokens, axis=0, keepdims=True)
+    rounded = (tokens * lax.rsqrt(mean + 1e-06)).astype(normed.dtype)
+    normed[...] = rounded
+    preact = over_features(rounded, up[...]) * up_scale
+    activation, slope = gelu_pair(preact)
+    slopes[...] = slope
+    hidden = activation.astype(mine.dtype)
+    halves_kept(core[0], hidden, mine, sent)
+    summed = lax.dot_general(
+        down[...], hidden, (((1,), (1,)), ((), ())), preferred_element_type=jnp.float32
+    )
+    partial[...] = (summed * down_scale).astype(partial.dtype)
+
+
+def forward(core, gathered, up, down, up_scale, down_scale):
+    features, tokens = gathered.shape
+    units = up.shape[1]
+    block = tokens // 4
+    by_feature = pl.BlockSpec((features, block), lambda i: (0, i))
+    by_half = pl.BlockSpec((block, units // 2), lambda i: (i, 0))
+    whole = pl.BlockSpec((features, units), lambda i: (0, 0))
     return pl.pallas_call(
-        functools.partial(gradient_kernel, scale=scale),
-        out_shape=jax.ShapeDtypeStruct((features, units), jnp.bfloat16),
-        grid=(features // block,),
-        in_specs=[
-            pl.BlockSpec((block, tokens), lambda i: (i, 0)),
-            pl.BlockSpec((tokens, units), lambda i: (0, 0)),
-            pl.BlockSpec((block, tokens), lambda i: (i + at[0], 0)),
-            pl.BlockSpec((tokens, units), lambda i: (0, at[1])),
-        ],
-        out_specs=pl.BlockSpec((block, units), lambda i: (i, 0)),
+        functools.partial(forward_kernel, up_scale=up_scale, down_scale=down_scale),
+        out_shape=(
+            jax.ShapeDtypeStruct((features, tokens), jnp.bfloat16),
+            jax.ShapeDtypeStruct((tokens, units // 2), jnp.bfloat16),
+            jax.ShapeDtypeStruct((tokens, units // 2), jnp.bfloat16),
+            jax.ShapeDtypeStruct((tokens, units), jnp.float32),
+            jax.ShapeDtypeStruct((features, tokens), jnp.bfloat16),
+        ),
+        grid=(tokens // block,),
+        in_specs=[pl.BlockSpec(memory_space=pltpu.SMEM), by_feature, whole, whole],
+        out_specs=(
+            by_feature,
+            by_half,
+            by_half,
+            pl.BlockSpec((block, units), lambda i: (i, 0)),
+            by_feature,
+        ),
         cost_estimate=pl.CostEstimate(
             flops=4 * features * tokens * units,
-            transcendentals=0,
-            bytes_accessed=4 * (features + units) * tokens + 2 * features * units,
+            transcendentals=tokens * units,
+            bytes_accessed=6 * features * tokens + 4 * features * units + 6 * tokens * units,
         ),
         compiler_params=pltpu.CompilerParams(dimension_semantics=("arbitrary",)),
-    )(first, first_units, second, second_units)
+        name="forward",
+    )(core.reshape(1), gathered, up, down)
 
 
 def hidden_kernel(core, piece, down, slopes, mine, sent, *, scale):
@@ -86,24 +116,13 @@
         piece[...], down[...], (((0,), (0,)), ((), ())), preferred_element_type=jnp.float32
     )
     rounded = (summed * scale * slopes[...]).astype(mine.dtype)
-    half = mine.shape[1]
-    low, high = rounded[:, :half], rounded[:, half:]
-
-    @pl.when(core[0] == 0)
-    def _():
-        mine[...] = low
-        sent[...] = high
-
-    @pl.when(core[0] != 0)
-    def _():
-        mine[...] = high
-        sent[...] = low
+    halves_kept(core[0], rounded, mine, sent)
 
 
 def hidden_gradient(core, piece, down, slopes, scale):
     features, tokens = piece.shape
     units = down.shape[1]
-    block = tokens // 4
+    block = tokens // 2
     half = jax.ShapeDtypeStruct((tokens, units // 2), jnp.bfloat16)
     return pl.pallas_call(
         functools.partial(hidden_kernel, scale=scale),
@@ -147,13 +166,26 @@
     return total
 
 
-def totals(first, second):
-    shape = (lax.axis_size(DP_MP), 128)
-    lane = lax.broadcasted_iota(jnp.int32, shape, 1)
-    rows = lax.all_to_all(
-        jnp.where(lane < 64, first, second), DP_MP, split_axis=0, concat_axis=0, tiled=True
-    )
-    summed = jnp.sum(rows, axis=0)
+def totals_kernel(loss, up, down, rows):
+    squares = jnp.sum(up[...] * up[...]) + jnp.sum(down[...] * down[...])
+    lane = lax.broadcasted_iota(jnp.int32, rows.shape, 2)
+    rows[...] = jnp.where(lane < 64, loss[0], squares)
+
+
+def totals(loss, up, down):
+    rows = pl.pallas_call(
+        totals_kernel,
+        out_shape=jax.ShapeDtypeStruct((lax.axis_size(DP_MP), 1, 128), jnp.float32),
+        in_specs=[
+            pl.BlockSpec(memory_space=pltpu.SMEM),
+            pl.BlockSpec(memory_space=pltpu.VMEM),
+            pl.BlockSpec(memory_space=pltpu.VMEM),
+        ],
+        out_specs=pl.BlockSpec(memory_space=pltpu.VMEM),
+        name="totals",
+    )(loss.reshape(1), up, down)
+    rows = lax.all_to_all(rows, DP_MP, split_axis=0, concat_axis=0, tiled=True)
+    summed = jnp.sum(rows, axis=(0, 1))
     return summed[0], summed[64]
 
 
@@ -235,11 +267,7 @@
     )
     latent_again = noisy_latent(*held[:2], alphas, sigmas)
     target = distill_target(latent_again, *held[2:], alphas, sigmas)
-    offset = latent_again - target
-    gathered_f = gathered.astype(jnp.float32)
-    normed = (
-        gathered_f * lax.rsqrt(jnp.mean(gathered_f * gathered_f, axis=0, keepdims=True) + 1e-06)
-    ).astype(jnp.bfloat16)
+    offset = (latent_again - target).reshape(row_count, width_local).T
     up_full, down_full = gathered_weights(
         up_master.astype(jnp.bfloat16), down_master.astype(jnp.bfloat16)
     )
@@ -247,51 +275,39 @@
     hidden_local = up_full.shape[1]
     dscale = width_full ** (-0.5)
     fscale = (hidden_local * lax.axis_size("mp")) ** (-0.5)
-    preact = over_features(normed, up_full) * dscale
-    activation, slopes = gelu_pair(preact)
-    hidden = activation.astype(jnp.bfloat16)
     core = lax.axis_index("c")
-    partial_value = (
-        lax.dot_general(
-            down_full, hidden, (((1,), (1,)), ((), ())), preferred_element_type=jnp.float32
-        )
-        * fscale
-    ).astype(jnp.bfloat16)
-    branch = lax.psum_scatter(partial_value, "mp", scatter_dimension=0, tiled=True).astype(
-        jnp.float32
-    )
-    offset, normed_other, hidden_mine, hidden_other = lax.optimization_barrier(
-        (
-            offset,
-            core_swapped(normed),
-            half_columns(hidden, core),
-            core_swapped(half_columns(hidden, 1 - core)),
-        )
-    )
-    errors = offset + branch.T.reshape(latent.shape)
-    weight_cube = weighting
-    loss_part = jnp.sum(weight_cube * errors * errors)
-    dpred = (
-        (2.0 * weight_cube / sample_total * errors)
-        .astype(jnp.bfloat16)
-        .reshape(row_count, width_local)
-    )
-    piece = lax.all_gather(dpred.T, "mp", axis=0, tiled=True)
+    normed, hidden_mine, hidden_sent, slopes, partial_value = forward(
+        core, gathered, up_full, down_full, dscale, fscale
+    )
+    branch = lax.psum_scatter(partial_value, "mp", scatter_dimension=0, tiled=True)
+    offset, normed_other, hidden_other = lax.optimization_barrier(
+        (offset, core_swapped(normed), core_swapped(hidden_sent))
+    )
+    weight_row = jnp.repeat(weighting.reshape(samples_dev), token_count)[None]
+    errors = offset + branch.astype(jnp.float32)
+    loss_part = jnp.sum(weight_row * errors * errors)
+    dpred = (2.0 * weight_row / sample_total * errors).astype(jnp.bfloat16)
+    piece = lax.all_gather(dpred, "mp", axis=0, tiled=True)
     piece_other = core_swapped(piece)
     dpre_mine, dpre_sent = hidden_gradient(core, piece, down_full, slopes, fscale)
     dpre_other = core_swapped(dpre_sent)
-    grad_down = weight_gradient(piece, hidden_mine, piece_other, hidden_other, (0, 0), fscale)
-    grad_up = weight_gradient(normed, dpre_mine, normed_other, dpre_other, (0, 0), dscale)
+    grad_down = (
+        jnp.dot(piece, hidden_mine, preferred_element_type=jnp.float32)
+        + jnp.dot(piece_other, hidden_other, preferred_element_type=jnp.float32)
+    ) * fscale
+    grad_up = (
+        jnp.dot(normed, dpre_mine, preferred_element_type=jnp.float32)
+        + jnp.dot(normed_other, dpre_other, preferred_element_type=jnp.float32)
+    ) * dscale
     chips = lax.axis_size(PLANE)
     rows_chip = width_full // chips
-    rows_down = from_plane(grad_down.reshape(chips, rows_chip, -1))
-    blocks_up = grad_up.reshape(
+    rows_down = from_plane(grad_down.astype(jnp.bfloat16).reshape(chips, rows_chip, -1))
+    blocks_up = grad_up.astype(jnp.bfloat16).reshape(
         lax.axis_size("y"), lax.axis_size("x"), rows_chip, -1
     )
     rows_up = from_axis(from_axis(jnp.swapaxes(blocks_up, 0, 1), "x"), "y")
     chip_rows = jnp.stack([rows_up, rows_down])
-    squares = jnp.sum(chip_rows * chip_rows)
-    loss_total, square_total = totals(loss_part, squares)
+    loss_total, square_total = totals(loss_part, rows_up, rows_down)
     by_core = chip_rows.reshape(2, 2, rows_chip // 2, -1)
     kept = lax.dynamic_index_in_dim(by_core, core, 1, keepdims=False)
     other = core_swapped(lax.dynamic_index_in_dim(by_core, 1 - core, 1, keepdims=False))

time: 282 us -> 271 us (0.961)
  other arithmetic: 18.9 us -> 10.9 us
  local copies, waits for them, and re-layouts: 14.6 us -> 7.4 us
  matrix products: 10.1 us -> 13.6 us
    reduce_sum x4 -> x1, other arithmetic: 5.52 us -> 0.29 us  [totals(): summed = jnp.sum(rows, axis=(0, 1))]
    dot_general x2 -> x4, matrix products: 10.1 us -> 13.6 us  [the longest x1 4.96 us: per_device(): jnp.dot(piece_other, hidden_other, preferred_element_type=jnp.float32)]
  transfers between devices with their start and end apart: 17 -> 17, of which waited for: 12 -> 11; matrix products, arithmetic and copies ran while one was open for 5% -> 6% of each run, Pallas kernels for 5% -> 3%
where the time goes in v3:
time: 271 us; the launch traced here: 267 us
  waiting for transfers between devices  133 us (49%)
  blocking collectives  37.1 us (14%)
  starting transfers between devices  25.3 us (9%)
  Pallas kernels  23.2 us (9%)
  between operations  16.6 us (6%)
  matrix products  13.6 us (5%)
  other arithmetic  10.9 us (4%)
  local copies, waits for them, and re-layouts  7.4 us (3%)
    all_gather x1, waiting for transfers between devices, per_device(): piece = lax.all_gather(dpred, 'mp', axis=0, tiled=True)  44.5 us
    reduce_scatter x1, waiting for transfers between devices, per_device(): lax.psum_scatter(partial_value, 'mp', scatter_dimension=0, tiled=True)  39.5 us
    all_to_all x1, blocking collectives, gathered_weights(): lax.all_to_all(jnp.broadcast_to(both, (chips,) + both.shape), PLANE, spli...  37.1 us
    ppermute x6, waiting for transfers between devices, from_axis(): lax.ppermute(sent.astype(jnp.bfloat16), axis, [(i, (i + step) % size) for...  28.1 us
    pallas_call x1, Pallas kernels, forward(): pl.pallas_call(functools.partial(forward_kernel, up_scale=up_scale, down_...  13.9 us
    all_to_all x1, waiting for transfers between devices, totals(): rows = lax.all_to_all(rows, DP_MP, split_axis=0, concat_axis=0, tiled=True)  11.3 us
    ppermute x6, waiting for transfers between devices, core_swapped(): return lax.ppermute(block, 'c', [(0, 1), (1, 0)])  9.48 us
    ppermute x6, starting transfers between devices, from_axis(): lax.ppermute(sent.astype(jnp.bfloat16), axis, [(i, (i + step) % size) for...  9.24 us
  transfers between devices with their start and end apart: 17, of which 11 were waited for; matrix products, arithmetic and copies ran while one was open for 6% of the time, Pallas kernels for 3%

profile of v3, /device:TPU:2, one launch (start us, length us, event | category | flops | bytes accessed | tf_op | source)
XLA Modules:
  0.0 267.5 jit_solution(13087655783531615058)
XLA Ops:
  11.2 37.1 %all_to_all.15 = bf16[16,96,768]{2,1,0:T(8,128)(2,1)S(1)} all-to-all(bf16[16,96,768]{2,1,0:T(8,128)(2,1)S(1)} %broadcast_in_dim.4), channel_id=1, replica_groups=mesh['y'=4,'x'=4,'c'=2,'mp'=8] {'y','x'}, dimensions={0} | all-to-all | bytes 4718592 | tf_op jit(solution)/shard_map/all_to_all | solution.py:39
  48.5 4.5 %collective-permute-done = bf16[16,96,768]{2,1,0:T(8,128)(2,1)} collective-permute-done((bf16[16,96,768]{2,1,0:T(8,128)(2,1)S(1)}, bf16[16,96,768]{2,1,0:T(8,128)(2,1)}, u32[]{:S(2)}, u32[]{:S(2)}) %collective-permute-start) | collective-permute-done | bytes 2359328 | tf_op jit(solution)/shard_map/ppermute | solution.py:26
  53.0 1.8 slice_bitcast_fusion
  55.2 1.6 copy.24
  59.0 13.9 %forward.1 = (bf16[1536,1024]{1,0:T(8,128)(2,1)}, bf16[1024,384]{1,0:T(8,128)(2,1)}, bf16[1024,384]{1,0:T(8,128)(2,1)}, f32[1024,768]{1,0:T(8,128)}, bf16[1536,1024]{1,0:T(8,128)(2,1)}) custom-call(s32[1]{0:T(128)} %bitcast.core, bf16[1536,1024]{1,0:T(8,128)(2,1)} %all-gather.3.cloned.1.call-done.gathered, bf16[1536,768]{1,0:T(8,128)(2,1)} %bitcast.111, ...), custom_call_target="tpu_custom_call" | custom-call | flops 4831838208 | bytes 18874368 | tf_op jit(solution)/shard_map/forward/pallas_call | solution.py:86
  75.3 5.0 %collective-permute-done.2 = bf16[1024,384]{1,0:T(8,128)(2,1)} collective-permute-done((bf16[1024,384]{1,0:T(8,128)(2,1)S(1)}, bf16[1024,384]{1,0:T(8,128)(2,1)}, u32[]{:S(2)}, u32[]{:S(2)}) %collective-permute-start.2) | collective-permute-done | bytes 786464 | tf_op jit(solution)/shard_map/ppermute | solution.py:26
  80.2 39.5 %reduce-scatter.2.cloned.1.call-done = bf16[192,1024]{1,0:T(8,128)(2,1)} async-done(((bf16[1536,1024]{1,0:T(8,128)(2,1)}), bf16[192,1024]{1,0:T(8,128)(2,1)}) %reduce-scatter.2.cloned.1.call-update) | async-done | bytes 393232 | tf_op jit(solution)/shard_map/reduce_scatter | solution.py:282
  119.8 2.5 multiply_convert_fusion
  122.3 44.5 %all-gather.5.cloned.1.call-done.piece = bf16[1536,1024]{1,0:T(8,128)(2,1)} async-done(((bf16[192,1024]{1,0:T(8,128)(2,1)}), bf16[1536,1024]{1,0:T(8,128)(2,1)}) %all-gather.5.cloned.1.call-update) | async-done | bytes 3145744 | tf_op jit(solution)/shard_map/all_gather | solution.py:290
  166.8 6.8 %hidden_gradient.1 = (bf16[1024,384]{1,0:T(8,128)(2,1)}, bf16[1024,384]{1,0:T(8,128)(2,1)}) custom-call(s32[1]{0:T(128)} %bitcast.core, bf16[1536,1024]{1,0:T(8,128)(2,1)} %all-gather.5.cloned.1.call-done.piece, bf16[1536,768]{1,0:T(8,128)(2,1)} %bitcast.110, f32[1024,768]{1,0:T(8,128)} %get-tuple-element.31.slopes), custom_call_target="tpu_custom_call" | custom-call | flops 2415919104 | bytes 10223616 | tf_op jit(solution)/shard_map/hidden_gradient/pallas_call | solution.py:127
  174.0 3.1 %fusion.41 = f32[1536,384]{1,0:T(8,128)S(1)} fusion(bf16[1536,1024]{1,0:T(8,128)(2,1)S(1)} %copy-done.12, bf16[1024,384]{1,0:T(8,128)(2,1)} %get-tuple-element.32), kind=kOutput, calls=%fused_computation.89 | convolution fusion | flops 1207959552 | bytes 6291456 | tf_op jit(solution)/shard_map/dot_general | solution.py:299
  177.1 1.8 fusion.42
  179.0 3.7 %fusion.2 = bf16[1536,384]{1,0:T(8,128)(2,1)S(1)} fusion(f32[1536,384]{1,0:T(8,128)S(1)} %fusion.41, bf16[1536,1024]{1,0:T(8,128)(2,1)} %collective-permute-done.1, bf16[1024,384]{1,0:T(8,128)(2,1)S(1)} %collective-permute-done.3), kind=kOutput, calls=%fused_computation.4 | convolution fusion | flops 1209729024 | bytes 7471104 | tf_op jit(solution)/shard_map/dot_general | solution.py:300
  182.7 5.0 %fusion.3 = bf16[1536,384]{1,0:T(8,128)(2,1)} fusion(f32[1536,384]{1,0:T(8,128)S(1)} %fusion.42, bf16[1536,1024]{1,0:T(8,128)(2,1)} %collective-permute-done.10, bf16[1024,384]{1,0:T(8,128)(2,1)} %collective-permute-done.2), kind=kOutput, calls=%fused_computation.5 | convolution fusion | flops 1209729024 | bytes 7471104 | tf_op jit(solution)/shard_map/dot_general | solution.py:296
  187.7 7.3 %all-to-all-start.1 = ((bf16[16,96,384]{2,1,0:T(8,128)(2,1)}), bf16[16,96,384]{2,1,0:T(8,128)(2,1)S(1)}, u32[]{:S(2)}, u32[]{:S(2)}) async-start(bf16[16,96,384]{2,1,0:T(8,128)(2,1)} %bitcast.25), calls=%async_computation.2 | async-start | bytes 2359296 | tf_op jit(solution)/shard_map/all_to_all | solution.py:152
  195.3 2.8 %collective-permute-start.5 = (bf16[4,96,384]{2,1,0:T(8,128)(2,1)S(1)}, bf16[4,96,384]{2,1,0:T(8,128)(2,1)}, u32[]{:S(2)}, u32[]{:S(2)}) collective-permute-start(bf16[4,96,384]{2,1,0:T(8,128)(2,1)S(1)} %get-tuple-element.51), channel_id=1, source_target_pairs={{0,32},{16,48},{32,0},{48,16},{1,33},{17,49},{33,1},{49,17},{2,34}... | collective-permute-start | bytes 884744 | tf_op jit(solution)/shard_map/ppermute | solution.py:162
  198.1 1.8 collective-permute-start.4
  199.8 16.9 %collective-permute-done.6 = bf16[4,96,384]{2,1,0:T(8,128)(2,1)} collective-permute-done((bf16[4,96,384]{2,1,0:T(8,128)(2,1)S(1)}, bf16[4,96,384]{2,1,0:T(8,128)(2,1)}, u32[]{:S(2)}, u32[]{:S(2)}) %collective-permute-start.6) | collective-permute-done | bytes 294944 | tf_op jit(solution)/shard_map/ppermute | solution.py:162
  216.7 6.2 %collective-permute-done.5 = bf16[4,96,384]{2,1,0:T(8,128)(2,1)} collective-permute-done((bf16[4,96,384]{2,1,0:T(8,128)(2,1)S(1)}, bf16[4,96,384]{2,1,0:T(8,128)(2,1)}, u32[]{:S(2)}, u32[]{:S(2)}) %collective-permute-start.5) | collective-permute-done | bytes 294944 | tf_op jit(solution)/shard_map/ppermute | solution.py:162
  224.3 2.8 %collective-permute-start.9 = (bf16[96,384]{1,0:T(8,128)(2,1)S(1)}, bf16[96,384]{1,0:T(8,128)(2,1)S(1)}, u32[]{:S(2)}, u32[]{:S(2)}) collective-permute-start(bf16[96,384]{1,0:T(8,128)(2,1)S(1)} %get-tuple-element.55), channel_id=1, source_target_pairs={{0,192},{64,0},{128,64},{192,128},{1,193},{65,1},{129,65},{193,129... | collective-permute-start | bytes 221192 | tf_op jit(solution)/shard_map/ppermute | solution.py:162
  229.5 3.5 %collective-permute-done.8 = bf16[96,384]{1,0:T(8,128)(2,1)S(1)} collective-permute-done((bf16[96,384]{1,0:T(8,128)(2,1)S(1)}, bf16[96,384]{1,0:T(8,128)(2,1)S(1)}, u32[]{:S(2)}, u32[]{:S(2)}) %collective-permute-start.8) | collective-permute-done | bytes 73760 | tf_op jit(solution)/shard_map/ppermute | solution.py:162
  234.6 2.5 totals.1
  237.1 8.0 %all-to-all-start.2 = ((f32[256,1,128]{2,1,0:T(1,128)}), f32[256,1,128]{2,1,0:T(1,128)S(1)}, u32[]{:S(2)}, u32[]{:S(2)}) async-start(f32[256,1,128]{2,1,0:T(1,128)} %totals.1), calls=%async_computation.3 | async-start | bytes 262144 | tf_op jit(solution)/shard_map/all_to_all | solution.py:187
  245.1 11.3 %all-to-all-done.2 = f32[256,1,128]{2,1,0:T(1,128)S(1)} async-done(((f32[256,1,128]{2,1,0:T(1,128)}), f32[256,1,128]{2,1,0:T(1,128)S(1)}, u32[]{:S(2)}, u32[]{:S(2)}) %all-to-all-start.2) | async-done | bytes 131104 | tf_op jit(solution)/shard_map/all_to_all | solution.py:187
  (85 shorter events, 17.1 us)
Async XLA Ops:
  7.2 3.8 %copy-start.4 = (f32[48,768]{1,0:T(8,128)S(1)}, f32[48,768]{1,0:T(8,128)}, u32[]{:S(2)}) copy-start(f32[48,768]{1,0:T(8,128)} %param.19) | copy-start | bytes 442372
  7.2 3.8 %copy-start.5 = (f32[48,768]{1,0:T(8,128)S(1)}, f32[48,768]{1,0:T(8,128)}, u32[]{:S(2)}) copy-start(f32[48,768]{1,0:T(8,128)} %param.18) | copy-start | bytes 442372
  7.2 51.8 %all-gather.3.cloned.1.call-start = ((), (), s32[]{:S(2)}) async-start(), calls=%async_computation.4 | async-start | bytes 3538944 | tf_op jit(solution)/shard_map/all_gather | solution.py:264
  10.9 108.9 %reduce-scatter.2.cloned.1.call-start = ((), (), s32[]{:S(2)}) async-start(), calls=%async_computation.5 | async-start | bytes 3538944 | tf_op jit(solution)/shard_map/reduce_scatter | solution.py:282
  48.3 4.7 %collective-permute-start = (bf16[16,96,768]{2,1,0:T(8,128)(2,1)S(1)}, bf16[16,96,768]{2,1,0:T(8,128)(2,1)}, u32[]{:S(2)}, u32[]{:S(2)}) collective-permute-start(bf16[16,96,768]{2,1,0:T(8,128)(2,1)S(1)} %all_to_all.15), channel_id=1, source_target_pairs={{0,8},{8,0},{1,9},{9,1},{2,10},{10,2},{3,11},{11,3},{4,12},{12,4},... | collective-permute-start | bytes 7077896 | tf_op jit(solution)/shard_map/ppermute | solution.py:26
  73.0 93.8 %all-gather.5.cloned.1.call-start = ((), (), s32[]{:S(2)}) async-start(), calls=%async_computation.6 | async-start | bytes 3538944 | tf_op jit(solution)/shard_map/all_gather | solution.py:290
  73.0 7.2 %collective-permute-start.1 = (bf16[1536,1024]{1,0:T(8,128)(2,1)}, bf16[1536,1024]{1,0:T(8,128)(2,1)}, u32[]{:S(2)}, u32[]{:S(2)}) collective-permute-start(bf16[1536,1024]{1,0:T(8,128)(2,1)} %get-tuple-element.23), channel_id=1, source_target_pairs={{0,8},{8,0},{1,9},{9,1},{2,10},{10,2},{3,11},{11,3},{4,12},{12,4},... | collective-permute-start | bytes 9437192 | tf_op jit(solution)/shard_map/ppermute | solution.py:26
  74.0 6.2 %collective-permute-start.2 = (bf16[1024,384]{1,0:T(8,128)(2,1)S(1)}, bf16[1024,384]{1,0:T(8,128)(2,1)}, u32[]{:S(2)}, u32[]{:S(2)}) collective-permute-start(bf16[1024,384]{1,0:T(8,128)(2,1)S(1)} %copy-done.14), channel_id=1, source_target_pairs={{0,8},{8,0},{1,9},{9,1},{2,10},{10,2},{3,11},{11,3},{4,12},{12,4},... | collective-permute-start | bytes 2359304 | tf_op jit(solution)/shard_map/ppermute | solution.py:26
  166.7 16.0 %collective-permute-start.10 = (bf16[1536,1024]{1,0:T(8,128)(2,1)}, bf16[1536,1024]{1,0:T(8,128)(2,1)}, u32[]{:S(2)}, u32[]{:S(2)}) collective-permute-start(bf16[1536,1024]{1,0:T(8,128)(2,1)} %all-gather.5.cloned.1.call-done.piece), channel_id=1, source_target_pairs={{0,8},{8,0},{1,9},{9,1},{2,10},{10,2},{3,11},{11,3},{4,12},{12,4},... | collective-permute-start | bytes 9437192 | tf_op jit(solution)/shard_map/ppermute | solution.py:26
  166.8 7.3 %copy-start.12 = (bf16[1536,1024]{1,0:T(8,128)(2,1)S(1)}, bf16[1536,1024]{1,0:T(8,128)(2,1)}, u32[]{:S(2)}) copy-start(bf16[1536,1024]{1,0:T(8,128)(2,1)} %get-tuple-element.23) | copy-start | bytes 9437188
  173.5 5.4 %collective-permute-start.3 = (bf16[1024,384]{1,0:T(8,128)(2,1)}, bf16[1024,384]{1,0:T(8,128)(2,1)S(1)}, u32[]{:S(2)}, u32[]{:S(2)}) collective-permute-start(bf16[1024,384]{1,0:T(8,128)(2,1)} %get-tuple-element.34), channel_id=1, source_target_pairs={{0,8},{8,0},{1,9},{9,1},{2,10},{10,2},{3,11},{11,3},{4,12},{12,4},... | collective-permute-start | bytes 2359304 | tf_op jit(solution)/shard_map/ppermute | solution.py:26
  187.7 46.1 %all-to-all-start.1 = ((bf16[16,96,384]{2,1,0:T(8,128)(2,1)}), bf16[16,96,384]{2,1,0:T(8,128)(2,1)S(1)}, u32[]{:S(2)}, u32[]{:S(2)}) async-start(bf16[16,96,384]{2,1,0:T(8,128)(2,1)} %bitcast.25), calls=%async_computation.2 | async-start | bytes 2359296 | tf_op jit(solution)/shard_map/all_to_all | solution.py:152
  195.1 21.7 %collective-permute-start.6 = (bf16[4,96,384]{2,1,0:T(8,128)(2,1)S(1)}, bf16[4,96,384]{2,1,0:T(8,128)(2,1)}, u32[]{:S(2)}, u32[]{:S(2)}) collective-permute-start(bf16[4,96,384]{2,1,0:T(8,128)(2,1)S(1)} %get-tuple-element.50), channel_id=1, source_target_pairs={{0,48},{16,0},{32,16},{48,32},{1,49},{17,1},{33,17},{49,33},{2,50}... | collective-permute-start | bytes 884744 | tf_op jit(solution)/shard_map/ppermute | solution.py:162
  195.3 27.7 %collective-permute-start.5 = (bf16[4,96,384]{2,1,0:T(8,128)(2,1)S(1)}, bf16[4,96,384]{2,1,0:T(8,128)(2,1)}, u32[]{:S(2)}, u32[]{:S(2)}) collective-permute-start(bf16[4,96,384]{2,1,0:T(8,128)(2,1)S(1)} %get-tuple-element.51), channel_id=1, source_target_pairs={{0,32},{16,48},{32,0},{48,16},{1,33},{17,49},{33,1},{49,17},{2,34}... | collective-permute-start | bytes 884744 | tf_op jit(solution)/shard_map/ppermute | solution.py:162
  198.1 24.9 %collective-permute-start.4 = (bf16[4,96,384]{2,1,0:T(8,128)(2,1)S(1)}, bf16[4,96,384]{2,1,0:T(8,128)(2,1)}, u32[]{:S(2)}, u32[]{:S(2)}) collective-permute-start(bf16[4,96,384]{2,1,0:T(8,128)(2,1)S(1)} %get-tuple-element.49), channel_id=1, source_target_pairs={{0,16},{16,32},{32,48},{48,0},{1,17},{17,33},{33,49},{49,1},{2,18}... | collective-permute-start | bytes 884744 | tf_op jit(solution)/shard_map/ppermute | solution.py:162
  224.2 34.5 %copy-start.8 = (f32[48,768]{1,0:T(8,128)S(1)}, f32[48,768]{1,0:T(8,128)}, u32[]{:S(2)}) copy-start(f32[48,768]{1,0:T(8,128)} %param.21) | copy-start | bytes 442372
  224.3 34.5 %copy-start.9 = (f32[48,768]{1,0:T(8,128)S(1)}, f32[48,768]{1,0:T(8,128)}, u32[]{:S(2)}) copy-start(f32[48,768]{1,0:T(8,128)} %param.23) | copy-start | bytes 442372
  224.3 34.5 %copy-start.10 = (f32[48,768]{1,0:T(8,128)S(1)}, f32[48,768]{1,0:T(8,128)}, u32[]{:S(2)}) copy-start(f32[48,768]{1,0:T(8,128)} %param.22) | copy-start | bytes 442372
  224.3 34.5 %copy-start.11 = (f32[48,768]{1,0:T(8,128)S(1)}, f32[48,768]{1,0:T(8,128)}, u32[]{:S(2)}) copy-start(f32[48,768]{1,0:T(8,128)} %param.20) | copy-start | bytes 442372
  224.3 5.2 %collective-permute-start.9 = (bf16[96,384]{1,0:T(8,128)(2,1)S(1)}, bf16[96,384]{1,0:T(8,128)(2,1)S(1)}, u32[]{:S(2)}, u32[]{:S(2)}) collective-permute-start(bf16[96,384]{1,0:T(8,128)(2,1)S(1)} %get-tuple-element.55), channel_id=1, source_target_pairs={{0,192},{64,0},{128,64},{192,128},{1,193},{65,1},{129,65},{193,129... | collective-permute-start | bytes 221192 | tf_op jit(solution)/shard_map/ppermute | solution.py:162
  227.1 5.9 %collective-permute-start.8 = (bf16[96,384]{1,0:T(8,128)(2,1)S(1)}, bf16[96,384]{1,0:T(8,128)(2,1)S(1)}, u32[]{:S(2)}, u32[]{:S(2)}) collective-permute-start(bf16[96,384]{1,0:T(8,128)(2,1)S(1)} %get-tuple-element.56), channel_id=1, source_target_pairs={{0,128},{64,192},{128,0},{192,64},{1,129},{65,193},{129,1},{193,65... | collective-permute-start | bytes 221192 | tf_op jit(solution)/shard_map/ppermute | solution.py:162
  227.9 5.8 %collective-permute-start.7 = (bf16[96,384]{1,0:T(8,128)(2,1)S(1)}, bf16[96,384]{1,0:T(8,128)(2,1)S(1)}, u32[]{:S(2)}, u32[]{:S(2)}) collective-permute-start(bf16[96,384]{1,0:T(8,128)(2,1)S(1)} %get-tuple-element.54), channel_id=1, source_target_pairs={{0,64},{64,128},{128,192},{192,0},{1,65},{65,129},{129,193},{193,1... | collective-permute-start | bytes 221192 | tf_op jit(solution)/shard_map/ppermute | solution.py:162
  234.0 11.1 %collective-permute-start.11 = (f32[2,48,384]{2,1,0:T(8,128)S(1)}, f32[2,48,384]{2,1,0:T(8,128)S(1)}, u32[]{:S(2)}, u32[]{:S(2)}) collective-permute-start(f32[2,48,384]{2,1,0:T(8,128)S(1)} %get-tuple-element.61), channel_id=1, source_target_pairs={{0,8},{8,0},{1,9},{9,1},{2,10},{10,2},{3,11},{11,3},{4,12},{12,4},... | collective-permute-start | bytes 442376 | tf_op jit(solution)/shard_map/ppermute | solution.py:26
  237.1 19.3 %all-to-all-start.2 = ((f32[256,1,128]{2,1,0:T(1,128)}), f32[256,1,128]{2,1,0:T(1,128)S(1)}, u32[]{:S(2)}, u32[]{:S(2)}) async-start(f32[256,1,128]{2,1,0:T(1,128)} %totals.1), calls=%async_computation.3 | async-start | bytes 262144 | tf_op jit(solution)/shard_map/all_to_all | solution.py:187
  (9 other events, 14.2 us)
Sparse Core Ops, SparseCore 0:
  11.0 47.9 all-gather.2
  73.1 46.6 reduce-scatter.1
  122.4 44.2 all-gather.4

commit v4 on v3

--- a/solution.py
+++ b/solution.py
@@ -148,15 +148,12 @@
     )(core.reshape(1), piece, down, slopes)
 
 
-def from_plane(halves):
-    parts = lax.all_to_all(halves, PLANE, split_axis=0, concat_axis=0, tiled=True)
-    return jnp.sum(parts.astype(jnp.float32), axis=0)
-
-
-def from_axis(blocks, axis):
+def from_axis(blocks, axis, after=None):
     size = lax.axis_size(axis)
     here = lax.axis_index(axis)
     total = lax.dynamic_index_in_dim(blocks, here, 0, keepdims=False).astype(jnp.float32)
+    if after is not None:
+        total, _ = lax.optimization_barrier((total, after))
     for step in range(1, size):
         sent = lax.dynamic_index_in_dim(blocks, (here + step) % size, 0, keepdims=False)
         moved = lax.ppermute(
@@ -204,11 +201,10 @@
 
 
 def rates(step_index, teacher_count):
-    steps_float = teacher_count.astype(jnp.float32)
-    doubled = 2.0 * step_index.astype(jnp.float32)
-    back = jnp.arange(3, dtype=jnp.float32)[:, None]
-    angles = 0.5 * math.pi * ((doubled - back) / steps_float)
-    return jnp.cos(angles)[:, :, None, None], jnp.sin(angles)[:, :, None, None]
+    steps_float = teacher_count.astype(jnp.float32)[:, None, None]
+    doubled = 2.0 * step_index.astype(jnp.float32)[:, None, None]
+    angles = [0.5 * math.pi * ((doubled - back) / steps_float) for back in (0.0, 1.0, 2.0)]
+    return [jnp.cos(angle) for angle in angles], [jnp.sin(angle) for angle in angles]
 
 
 def noisy_latent(clean, noise, alphas, sigmas):
@@ -285,9 +281,13 @@
     )
     weight_row = jnp.repeat(weighting.reshape(samples_dev), token_count)[None]
     errors = offset + branch.astype(jnp.float32)
+    dpred = (2.0 * weight_row / sample_total * errors).astype(jnp.bfloat16)
+    offset, branch, dpred = lax.optimization_barrier((offset, branch, dpred))
+    errors = offset + branch.astype(jnp.float32)
     loss_part = jnp.sum(weight_row * errors * errors)
-    dpred = (2.0 * weight_row / sample_total * errors).astype(jnp.bfloat16)
-    piece = lax.all_gather(dpred, "mp", axis=0, tiled=True)
+    piece, loss_part = lax.optimization_barrier(
+        (lax.all_gather(dpred, "mp", axis=0, tiled=True), loss_part)
+    )
     piece_other = core_swapped(piece)
     dpre_mine, dpre_sent = hidden_gradient(core, piece, down_full, slopes, fscale)
     dpre_other = core_swapped(dpre_sent)
@@ -299,16 +299,15 @@
         jnp.dot(normed, dpre_mine, preferred_element_type=jnp.float32)
         + jnp.dot(normed_other, dpre_other, preferred_element_type=jnp.float32)
     ) * dscale
-    chips = lax.axis_size(PLANE)
-    rows_chip = width_full // chips
-    rows_down = from_plane(grad_down.astype(jnp.bfloat16).reshape(chips, rows_chip, -1))
-    blocks_up = grad_up.astype(jnp.bfloat16).reshape(
-        lax.axis_size("y"), lax.axis_size("x"), rows_chip, -1
-    )
-    rows_up = from_axis(from_axis(jnp.swapaxes(blocks_up, 0, 1), "x"), "y")
+    blocks = (lax.axis_size("y"), lax.axis_size("x"), width_full // lax.axis_size(PLANE), -1)
+    sums_down = from_axis(grad_down.astype(jnp.bfloat16).reshape(blocks), "y")
+    rows_down = from_axis(sums_down, "x")
+    blocks_up = jnp.swapaxes(grad_up.astype(jnp.bfloat16).reshape(blocks), 0, 1)
+    sums_up = from_axis(blocks_up, "x", rows_down)
+    rows_up = from_axis(sums_up, "y")
     chip_rows = jnp.stack([rows_up, rows_down])
     loss_total, square_total = totals(loss_part, rows_up, rows_down)
-    by_core = chip_rows.reshape(2, 2, rows_chip // 2, -1)
+    by_core = chip_rows.reshape(2, 2, blocks[2] // 2, -1)
     kept = lax.dynamic_index_in_dim(by_core, core, 1, keepdims=False)
     other = core_swapped(lax.dynamic_index_in_dim(by_core, 1 - core, 1, keepdims=False))
     mine_up, mine_down = jnp.where(

time: 271 us -> 268 us (0.989)
    all_to_all x1 -> x0, starting transfers between devices: 7.27 us -> none  [from_plane(): lax.all_to_all(halves, PLANE, split_axis=0, concat_axis=0, tiled=True)]
    ppermute x6 -> x12, starting transfers between devices: 9.24 us -> 15.8 us  [from_axis(): lax.ppermute(sent.astype(jnp.bfloat16), axis, [(i, (i + step) % size) for...]
    ppermute x6 -> x12, waiting for transfers between devices: 28.1 us -> 28.1 us  [from_axis(): lax.ppermute(sent.astype(jnp.bfloat16), axis, [(i, (i + step) % size) for...]
  transfers between devices with their start and end apart: 17 -> 22, of which waited for: 11 -> 13; matrix products, arithmetic and copies ran while one was open for 6% -> 8% of each run, Pallas kernels for 3% -> 4%
where the time goes in v4:
time: 268 us; the launch traced here: 265 us
  waiting for transfers between devices  132 us (49%)
  blocking collectives  37.1 us (14%)
  starting transfers between devices  25.6 us (10%)
  Pallas kernels  23.2 us (9%)
  between operations  16.7 us (6%)
  matrix products  12.6 us (5%)
  other arithmetic  10.4 us (4%)
  local copies, waits for them, and re-layouts  7.44 us (3%)
    all_gather x1, waiting for transfers between devices, per_device(): lax.all_gather(dpred, 'mp', axis=0, tiled=True)  42.7 us
    reduce_scatter x1, waiting for transfers between devices, per_device(): lax.psum_scatter(partial_value, 'mp', scatter_dimension=0, tiled=True)  39.5 us
    all_to_all x1, blocking collectives, gathered_weights(): lax.all_to_all(jnp.broadcast_to(both, (chips,) + both.shape), PLANE, spli...  37.1 us
    ppermute x12, waiting for transfers between devices, from_axis(): lax.ppermute(sent.astype(jnp.bfloat16), axis, [(i, (i + step) % size) for...  28.1 us
    ppermute x12, starting transfers between devices, from_axis(): lax.ppermute(sent.astype(jnp.bfloat16), axis, [(i, (i + step) % size) for...  15.8 us
    pallas_call x1, Pallas kernels, forward(): pl.pallas_call(functools.partial(forward_kernel, up_scale=up_scale, down_...  13.9 us
    all_to_all x1, waiting for transfers between devices, totals(): rows = lax.all_to_all(rows, DP_MP, split_axis=0, concat_axis=0, tiled=True)  11.3 us
    ppermute x6, waiting for transfers between devices, core_swapped(): return lax.ppermute(block, 'c', [(0, 1), (1, 0)])  9.47 us
  transfers between devices with their start and end apart: 22, of which 13 were waited for; matrix products, arithmetic and copies ran while one was open for 8% of the time, Pallas kernels for 4%

profile of v4, /device:TPU:2, one launch (start us, length us, event | category | flops | bytes accessed | tf_op | source)
XLA Modules:
  0.0 264.7 jit_solution(6219464501743893808)
XLA Ops:
  10.6 37.1 %all_to_all.10 = bf16[16,96,768]{2,1,0:T(8,128)(2,1)S(1)} all-to-all(bf16[16,96,768]{2,1,0:T(8,128)(2,1)S(1)} %broadcast_in_dim.8), channel_id=1, replica_groups=mesh['y'=4,'x'=4,'c'=2,'mp'=8] {'y','x'}, dimensions={0} | all-to-all | bytes 4718592 | tf_op jit(solution)/shard_map/all_to_all | solution.py:39
  47.9 4.5 %collective-permute-done = bf16[16,96,768]{2,1,0:T(8,128)(2,1)} collective-permute-done((bf16[16,96,768]{2,1,0:T(8,128)(2,1)S(1)}, bf16[16,96,768]{2,1,0:T(8,128)(2,1)}, u32[]{:S(2)}, u32[]{:S(2)}) %collective-permute-start) | collective-permute-done | bytes 2359328 | tf_op jit(solution)/shard_map/ppermute | solution.py:26
  58.4 13.9 %forward.1 = (bf16[1536,1024]{1,0:T(8,128)(2,1)}, bf16[1024,384]{1,0:T(8,128)(2,1)}, bf16[1024,384]{1,0:T(8,128)(2,1)}, f32[1024,768]{1,0:T(8,128)}, bf16[1536,1024]{1,0:T(8,128)(2,1)}) custom-call(s32[1]{0:T(128)} %bitcast.core, bf16[1536,1024]{1,0:T(8,128)(2,1)} %all-gather.3.cloned.1.call-done.gathered, bf16[1536,768]{1,0:T(8,128)(2,1)} %bitcast.107, ...), custom_call_target="tpu_custom_call" | custom-call | flops 4831838208 | bytes 18874368 | tf_op jit(solution)/shard_map/forward/pallas_call | solution.py:86
  74.7 5.0 %collective-permute-done.2 = bf16[1024,384]{1,0:T(8,128)(2,1)} collective-permute-done((bf16[1024,384]{1,0:T(8,128)(2,1)S(1)}, bf16[1024,384]{1,0:T(8,128)(2,1)}, u32[]{:S(2)}, u32[]{:S(2)}) %collective-permute-start.2) | collective-permute-done | bytes 786464 | tf_op jit(solution)/shard_map/ppermute | solution.py:26
  79.6 39.5 %reduce-scatter.2.cloned.1.call-done = bf16[192,1024]{1,0:T(8,128)(2,1)} async-done(((bf16[1536,1024]{1,0:T(8,128)(2,1)}), bf16[192,1024]{1,0:T(8,128)(2,1)}) %reduce-scatter.2.cloned.1.call-update) | async-done | bytes 393232 | tf_op jit(solution)/shard_map/reduce_scatter | solution.py:278
  119.1 1.9 multiply_convert_fusion
  121.0 1.8 fusion.16
  122.8 42.7 %all-gather.5.cloned.1.call-done.piece = bf16[1536,1024]{1,0:T(8,128)(2,1)} async-done(((bf16[192,1024]{1,0:T(8,128)(2,1)}), bf16[1536,1024]{1,0:T(8,128)(2,1)}) %all-gather.5.cloned.1.call-update) | async-done | bytes 3145744 | tf_op jit(solution)/shard_map/all_gather | solution.py:289
  165.5 6.8 %hidden_gradient.1 = (bf16[1024,384]{1,0:T(8,128)(2,1)}, bf16[1024,384]{1,0:T(8,128)(2,1)}) custom-call(s32[1]{0:T(128)} %bitcast.core, bf16[1536,1024]{1,0:T(8,128)(2,1)} %all-gather.5.cloned.1.call-done.piece, bf16[1536,768]{1,0:T(8,128)(2,1)} %bitcast.106, f32[1024,768]{1,0:T(8,128)} %get-tuple-element.41.slopes), custom_call_target="tpu_custom_call" | custom-call | flops 2415919104 | bytes 10223616 | tf_op jit(solution)/shard_map/hidden_gradient/pallas_call | solution.py:127
  172.8 3.1 %fusion.51 = f32[1536,384]{1,0:T(8,128)S(1)} fusion(bf16[1536,1024]{1,0:T(8,128)(2,1)S(1)} %copy-done.12, bf16[1024,384]{1,0:T(8,128)(2,1)} %get-tuple-element.42), kind=kOutput, calls=%fused_computation.100 | convolution fusion | flops 1207959552 | bytes 6291456 | tf_op jit(solution)/shard_map/dot_general | solution.py:299
  175.9 1.8 fusion.52
  177.8 3.9 %fusion.3 = bf16[1536,384]{1,0:T(8,128)(2,1)S(1)} fusion(f32[1536,384]{1,0:T(8,128)S(1)} %fusion.52, bf16[1536,1024]{1,0:T(8,128)(2,1)} %collective-permute-done.4, bf16[1024,384]{1,0:T(8,128)(2,1)} %collective-permute-done.2), kind=kOutput, calls=%fused_computation.5 | convolution fusion | flops 1209729024 | bytes 7471104 | tf_op jit(solution)/shard_map/dot_general | solution.py:296
  181.8 2.8 %collective-permute-start.7 = (bf16[4,96,384]{2,1,0:T(8,128)(2,1)S(1)}, bf16[4,96,384]{2,1,0:T(8,128)(2,1)S(1)}, u32[]{:S(2)}, u32[]{:S(2)}) collective-permute-start(bf16[4,96,384]{2,1,0:T(8,128)(2,1)S(1)} %get-tuple-element.72), channel_id=1, source_target_pairs={{0,192},{64,0},{128,64},{192,128},{1,193},{65,1},{129,65},{193,129... | collective-permute-start | bytes 884744 | tf_op jit(solution)/shard_map/ppermute | solution.py:159
  186.3 3.7 %fusion.2 = bf16[1536,384]{1,0:T(8,128)(2,1)S(1)} fusion(f32[1536,384]{1,0:T(8,128)S(1)} %fusion.51, bf16[1536,1024]{1,0:T(8,128)(2,1)} %collective-permute-done.1, bf16[1024,384]{1,0:T(8,128)(2,1)S(1)} %collective-permute-done.3), kind=kOutput, calls=%fused_computation.4 | convolution fusion | flops 1209729024 | bytes 7471104 | tf_op jit(solution)/shard_map/dot_general | solution.py:300
  190.0 7.4 %collective-permute-done.7 = bf16[4,96,384]{2,1,0:T(8,128)(2,1)S(1)} collective-permute-done((bf16[4,96,384]{2,1,0:T(8,128)(2,1)S(1)}, bf16[4,96,384]{2,1,0:T(8,128)(2,1)S(1)}, u32[]{:S(2)}, u32[]{:S(2)}) %collective-permute-start.7) | collective-permute-done | bytes 294944 | tf_op jit(solution)/shard_map/ppermute | solution.py:159
  197.4 3.7 %collective-permute-done.5 = bf16[4,96,384]{2,1,0:T(8,128)(2,1)S(1)} collective-permute-done((bf16[4,96,384]{2,1,0:T(8,128)(2,1)S(1)}, bf16[4,96,384]{2,1,0:T(8,128)(2,1)S(1)}, u32[]{:S(2)}, u32[]{:S(2)}) %collective-permute-start.5) | collective-permute-done | bytes 294944 | tf_op jit(solution)/shard_map/ppermute | solution.py:159
  201.9 2.4 collective-permute-start.9
  207.8 2.5 collective-permute-start.11
  210.5 10.4 %collective-permute-done.13 = bf16[4,96,384]{2,1,0:T(8,128)(2,1)S(1)} collective-permute-done((bf16[4,96,384]{2,1,0:T(8,128)(2,1)S(1)}, bf16[4,96,384]{2,1,0:T(8,128)(2,1)S(1)}, u32[]{:S(2)}, u32[]{:S(2)}) %collective-permute-start.13) | collective-permute-done | bytes 294944 | tf_op jit(solution)/shard_map/ppermute | solution.py:159
  225.0 2.1 collective-permute-done.16
  227.1 2.5 collective-permute-done.15
  230.7 2.5 totals.1
  233.3 9.1 %all-to-all-start.1 = ((f32[256,1,128]{2,1,0:T(1,128)}), f32[256,1,128]{2,1,0:T(1,128)S(1)}, u32[]{:S(2)}, u32[]{:S(2)}) async-start(f32[256,1,128]{2,1,0:T(1,128)} %totals.1), calls=%async_computation.2 | async-start | bytes 262144 | tf_op jit(solution)/shard_map/all_to_all | solution.py:184
  242.4 11.3 %all-to-all-done.1 = f32[256,1,128]{2,1,0:T(1,128)S(1)} async-done(((f32[256,1,128]{2,1,0:T(1,128)}), f32[256,1,128]{2,1,0:T(1,128)S(1)}, u32[]{:S(2)}, u32[]{:S(2)}) %all-to-all-start.1) | async-done | bytes 131104 | tf_op jit(solution)/shard_map/all_to_all | solution.py:184
  (99 shorter events, 25.7 us)
Async XLA Ops:
  7.2 51.2 %all-gather.3.cloned.1.call-start = ((), (), s32[]{:S(2)}) async-start(), calls=%async_computation.3 | async-start | bytes 3538944 | tf_op jit(solution)/shard_map/all_gather | solution.py:260
  10.3 108.9 %reduce-scatter.2.cloned.1.call-start = ((), (), s32[]{:S(2)}) async-start(), calls=%async_computation.4 | async-start | bytes 3538944 | tf_op jit(solution)/shard_map/reduce_scatter | solution.py:278
  47.7 4.7 %collective-permute-start = (bf16[16,96,768]{2,1,0:T(8,128)(2,1)S(1)}, bf16[16,96,768]{2,1,0:T(8,128)(2,1)}, u32[]{:S(2)}, u32[]{:S(2)}) collective-permute-start(bf16[16,96,768]{2,1,0:T(8,128)(2,1)S(1)} %all_to_all.10), channel_id=1, source_target_pairs={{0,8},{8,0},{1,9},{9,1},{2,10},{10,2},{3,11},{11,3},{4,12},{12,4},... | collective-permute-start | bytes 7077896 | tf_op jit(solution)/shard_map/ppermute | solution.py:26
  72.4 93.1 %all-gather.5.cloned.1.call-start = ((), (), s32[]{:S(2)}) async-start(), calls=%async_computation.5 | async-start | bytes 3538944 | tf_op jit(solution)/shard_map/all_gather | solution.py:289
  72.4 7.2 %collective-permute-start.1 = (bf16[1536,1024]{1,0:T(8,128)(2,1)}, bf16[1536,1024]{1,0:T(8,128)(2,1)}, u32[]{:S(2)}, u32[]{:S(2)}) collective-permute-start(bf16[1536,1024]{1,0:T(8,128)(2,1)} %get-tuple-element.29), channel_id=1, source_target_pairs={{0,8},{8,0},{1,9},{9,1},{2,10},{10,2},{3,11},{11,3},{4,12},{12,4},... | collective-permute-start | bytes 9437192 | tf_op jit(solution)/shard_map/ppermute | solution.py:26
  73.4 6.2 %collective-permute-start.2 = (bf16[1024,384]{1,0:T(8,128)(2,1)S(1)}, bf16[1024,384]{1,0:T(8,128)(2,1)}, u32[]{:S(2)}, u32[]{:S(2)}) collective-permute-start(bf16[1024,384]{1,0:T(8,128)(2,1)S(1)} %copy-done.14), channel_id=1, source_target_pairs={{0,8},{8,0},{1,9},{9,1},{2,10},{10,2},{3,11},{11,3},{4,12},{12,4},... | collective-permute-start | bytes 2359304 | tf_op jit(solution)/shard_map/ppermute | solution.py:26
  165.5 12.2 %collective-permute-start.4 = (bf16[1536,1024]{1,0:T(8,128)(2,1)}, bf16[1536,1024]{1,0:T(8,128)(2,1)}, u32[]{:S(2)}, u32[]{:S(2)}) collective-permute-start(bf16[1536,1024]{1,0:T(8,128)(2,1)} %all-gather.5.cloned.1.call-done.piece), channel_id=1, source_target_pairs={{0,8},{8,0},{1,9},{9,1},{2,10},{10,2},{3,11},{11,3},{4,12},{12,4},... | collective-permute-start | bytes 9437192 | tf_op jit(solution)/shard_map/ppermute | solution.py:26
  172.3 14.0 %collective-permute-start.3 = (bf16[1024,384]{1,0:T(8,128)(2,1)}, bf16[1024,384]{1,0:T(8,128)(2,1)S(1)}, u32[]{:S(2)}, u32[]{:S(2)}) collective-permute-start(bf16[1024,384]{1,0:T(8,128)(2,1)} %get-tuple-element.44), channel_id=1, source_target_pairs={{0,8},{8,0},{1,9},{9,1},{2,10},{10,2},{3,11},{11,3},{4,12},{12,4},... | collective-permute-start | bytes 2359304 | tf_op jit(solution)/shard_map/ppermute | solution.py:26
  181.8 15.6 %collective-permute-start.7 = (bf16[4,96,384]{2,1,0:T(8,128)(2,1)S(1)}, bf16[4,96,384]{2,1,0:T(8,128)(2,1)S(1)}, u32[]{:S(2)}, u32[]{:S(2)}) collective-permute-start(bf16[4,96,384]{2,1,0:T(8,128)(2,1)S(1)} %get-tuple-element.72), channel_id=1, source_target_pairs={{0,192},{64,0},{128,64},{192,128},{1,193},{65,1},{129,65},{193,129... | collective-permute-start | bytes 884744 | tf_op jit(solution)/shard_map/ppermute | solution.py:159
  184.6 12.8 %collective-permute-start.6 = (bf16[4,96,384]{2,1,0:T(8,128)(2,1)S(1)}, bf16[4,96,384]{2,1,0:T(8,128)(2,1)S(1)}, u32[]{:S(2)}, u32[]{:S(2)}) collective-permute-start(bf16[4,96,384]{2,1,0:T(8,128)(2,1)S(1)} %get-tuple-element.73), channel_id=1, source_target_pairs={{0,128},{64,192},{128,0},{192,64},{1,129},{65,193},{129,1},{193,65... | collective-permute-start | bytes 884744 | tf_op jit(solution)/shard_map/ppermute | solution.py:159
  185.4 15.7 %collective-permute-start.5 = (bf16[4,96,384]{2,1,0:T(8,128)(2,1)S(1)}, bf16[4,96,384]{2,1,0:T(8,128)(2,1)S(1)}, u32[]{:S(2)}, u32[]{:S(2)}) collective-permute-start(bf16[4,96,384]{2,1,0:T(8,128)(2,1)S(1)} %get-tuple-element.71), channel_id=1, source_target_pairs={{0,64},{64,128},{128,192},{192,0},{1,65},{65,129},{129,193},{193,1... | collective-permute-start | bytes 884744 | tf_op jit(solution)/shard_map/ppermute | solution.py:159
  201.3 6.6 %collective-permute-start.10 = (bf16[96,384]{1,0:T(8,128)(2,1)S(1)}, bf16[96,384]{1,0:T(8,128)(2,1)S(1)}, u32[]{:S(2)}, u32[]{:S(2)}) collective-permute-start(bf16[96,384]{1,0:T(8,128)(2,1)S(1)} %get-tuple-element.78), channel_id=1, source_target_pairs={{0,48},{16,0},{32,16},{48,32},{1,49},{17,1},{33,17},{49,33},{2,50}... | collective-permute-start | bytes 221192 | tf_op jit(solution)/shard_map/ppermute | solution.py:159
  201.9 8.5 %collective-permute-start.9 = (bf16[96,384]{1,0:T(8,128)(2,1)S(1)}, bf16[96,384]{1,0:T(8,128)(2,1)S(1)}, u32[]{:S(2)}, u32[]{:S(2)}) collective-permute-start(bf16[96,384]{1,0:T(8,128)(2,1)S(1)} %get-tuple-element.79), channel_id=1, source_target_pairs={{0,32},{16,48},{32,0},{48,16},{1,33},{17,49},{33,1},{49,17},{2,34}... | collective-permute-start | bytes 221192 | tf_op jit(solution)/shard_map/ppermute | solution.py:159
  204.3 6.1 %collective-permute-start.8 = (bf16[96,384]{1,0:T(8,128)(2,1)S(1)}, bf16[96,384]{1,0:T(8,128)(2,1)S(1)}, u32[]{:S(2)}, u32[]{:S(2)}) collective-permute-start(bf16[96,384]{1,0:T(8,128)(2,1)S(1)} %get-tuple-element.77), channel_id=1, source_target_pairs={{0,16},{16,32},{32,48},{48,0},{1,17},{17,33},{33,49},{49,1},{2,18}... | collective-permute-start | bytes 221192 | tf_op jit(solution)/shard_map/ppermute | solution.py:159
  206.2 14.7 %collective-permute-start.13 = (bf16[4,96,384]{2,1,0:T(8,128)(2,1)S(1)}, bf16[4,96,384]{2,1,0:T(8,128)(2,1)S(1)}, u32[]{:S(2)}, u32[]{:S(2)}) collective-permute-start(bf16[4,96,384]{2,1,0:T(8,128)(2,1)S(1)} %get-tuple-element.68), channel_id=1, source_target_pairs={{0,48},{16,0},{32,16},{48,32},{1,49},{17,1},{33,17},{49,33},{2,50}... | collective-permute-start | bytes 884744 | tf_op jit(solution)/shard_map/ppermute | solution.py:159
  206.5 14.4 %collective-permute-start.12 = (bf16[4,96,384]{2,1,0:T(8,128)(2,1)S(1)}, bf16[4,96,384]{2,1,0:T(8,128)(2,1)S(1)}, u32[]{:S(2)}, u32[]{:S(2)}) collective-permute-start(bf16[4,96,384]{2,1,0:T(8,128)(2,1)S(1)} %get-tuple-element.69), channel_id=1, source_target_pairs={{0,32},{16,48},{32,0},{48,16},{1,33},{17,49},{33,1},{49,17},{2,34}... | collective-permute-start | bytes 884744 | tf_op jit(solution)/shard_map/ppermute | solution.py:159
  207.8 14.7 %collective-permute-start.11 = (bf16[4,96,384]{2,1,0:T(8,128)(2,1)S(1)}, bf16[4,96,384]{2,1,0:T(8,128)(2,1)S(1)}, u32[]{:S(2)}, u32[]{:S(2)}) collective-permute-start(bf16[4,96,384]{2,1,0:T(8,128)(2,1)S(1)} %get-tuple-element.67), channel_id=1, source_target_pairs={{0,16},{16,32},{32,48},{48,0},{1,17},{17,33},{33,49},{49,1},{2,18}... | collective-permute-start | bytes 884744 | tf_op jit(solution)/shard_map/ppermute | solution.py:159
  210.4 45.5 %copy-start.8 = (f32[48,768]{1,0:T(8,128)S(1)}, f32[48,768]{1,0:T(8,128)}, u32[]{:S(2)}) copy-start(f32[48,768]{1,0:T(8,128)} %param.21) | copy-start | bytes 442372
  210.4 45.5 %copy-start.9 = (f32[48,768]{1,0:T(8,128)S(1)}, f32[48,768]{1,0:T(8,128)}, u32[]{:S(2)}) copy-start(f32[48,768]{1,0:T(8,128)} %param.23) | copy-start | bytes 442372
  222.7 4.4 %collective-permute-start.16 = (bf16[96,384]{1,0:T(8,128)(2,1)S(1)}, bf16[96,384]{1,0:T(8,128)(2,1)S(1)}, u32[]{:S(2)}, u32[]{:S(2)}) collective-permute-start(bf16[96,384]{1,0:T(8,128)(2,1)S(1)} %get-tuple-element.75), channel_id=1, source_target_pairs={{0,192},{64,0},{128,64},{192,128},{1,193},{65,1},{129,65},{193,129... | collective-permute-start | bytes 221192 | tf_op jit(solution)/shard_map/ppermute | solution.py:159
  222.8 6.8 %collective-permute-start.15 = (bf16[96,384]{1,0:T(8,128)(2,1)S(1)}, bf16[96,384]{1,0:T(8,128)(2,1)S(1)}, u32[]{:S(2)}, u32[]{:S(2)}) collective-permute-start(bf16[96,384]{1,0:T(8,128)(2,1)S(1)} %get-tuple-element.76), channel_id=1, source_target_pairs={{0,128},{64,192},{128,0},{192,64},{1,129},{65,193},{129,1},{193,65... | collective-permute-start | bytes 221192 | tf_op jit(solution)/shard_map/ppermute | solution.py:159
  223.7 6.4 %collective-permute-start.14 = (bf16[96,384]{1,0:T(8,128)(2,1)S(1)}, bf16[96,384]{1,0:T(8,128)(2,1)S(1)}, u32[]{:S(2)}, u32[]{:S(2)}) collective-permute-start(bf16[96,384]{1,0:T(8,128)(2,1)S(1)} %get-tuple-element.74), channel_id=1, source_target_pairs={{0,64},{64,128},{128,192},{192,0},{1,65},{65,129},{129,193},{193,1... | collective-permute-start | bytes 221192 | tf_op jit(solution)/shard_map/ppermute | solution.py:159
  230.1 12.2 %collective-permute-start.17 = (f32[2,48,384]{2,1,0:T(8,128)S(1)}, f32[2,48,384]{2,1,0:T(8,128)S(1)}, u32[]{:S(2)}, u32[]{:S(2)}) collective-permute-start(f32[2,48,384]{2,1,0:T(8,128)S(1)} %get-tuple-element.84), channel_id=1, source_target_pairs={{0,8},{8,0},{1,9},{9,1},{2,10},{10,2},{3,11},{11,3},{4,12},{12,4},... | collective-permute-start | bytes 442376 | tf_op jit(solution)/shard_map/ppermute | solution.py:26
  233.3 20.5 %all-to-all-start.1 = ((f32[256,1,128]{2,1,0:T(1,128)}), f32[256,1,128]{2,1,0:T(1,128)S(1)}, u32[]{:S(2)}, u32[]{:S(2)}) async-start(f32[256,1,128]{2,1,0:T(1,128)} %totals.1), calls=%async_computation.2 | async-start | bytes 262144 | tf_op jit(solution)/shard_map/all_to_all | solution.py:184
  (14 other events, 138.1 us)
Sparse Core Ops, SparseCore 0:
  10.4 47.9 all-gather.2
  72.5 46.6 reduce-scatter.1
  121.1 44.3 all-gather.4

commit v5 on v4

--- a/solution.py
+++ b/solution.py
@@ -28,7 +28,9 @@
 
 def core_joined(mine, other):
     first = lax.axis_index("c") == 0
-    pair = jnp.where(first, jnp.stack([mine, other], 1), jnp.stack([other, mine], 1))
+    pair = jnp.where(
+        first, jnp.concatenate([mine, other], axis=1), jnp.concatenate([other, mine], axis=1)
+    )
     return pair.reshape(-1, mine.shape[-1])
 
 
@@ -163,27 +165,10 @@
     return total
 
 
-def totals_kernel(loss, up, down, rows):
-    squares = jnp.sum(up[...] * up[...]) + jnp.sum(down[...] * down[...])
-    lane = lax.broadcasted_iota(jnp.int32, rows.shape, 2)
-    rows[...] = jnp.where(lane < 64, loss[0], squares)
-
-
-def totals(loss, up, down):
-    rows = pl.pallas_call(
-        totals_kernel,
-        out_shape=jax.ShapeDtypeStruct((lax.axis_size(DP_MP), 1, 128), jnp.float32),
-        in_specs=[
-            pl.BlockSpec(memory_space=pltpu.SMEM),
-            pl.BlockSpec(memory_space=pltpu.VMEM),
-            pl.BlockSpec(memory_space=pltpu.VMEM),
-        ],
-        out_specs=pl.BlockSpec(memory_space=pltpu.VMEM),
-        name="totals",
-    )(loss.reshape(1), up, down)
+def total(value):
+    rows = jnp.broadcast_to(value, (lax.axis_size(DP_MP), 1, 128))
     rows = lax.all_to_all(rows, DP_MP, split_axis=0, concat_axis=0, tiled=True)
-    summed = jnp.sum(rows, axis=(0, 1))
-    return summed[0], summed[64]
+    return jnp.sum(rows, axis=0)
 
 
 def over_features(left, right):
@@ -285,8 +270,8 @@
     offset, branch, dpred = lax.optimization_barrier((offset, branch, dpred))
     errors = offset + branch.astype(jnp.float32)
     loss_part = jnp.sum(weight_row * errors * errors)
-    piece, loss_part = lax.optimization_barrier(
-        (lax.all_gather(dpred, "mp", axis=0, tiled=True), loss_part)
+    piece, loss_total = lax.optimization_barrier(
+        (lax.all_gather(dpred, "mp", axis=0, tiled=True), total(loss_part))
     )
     piece_other = core_swapped(piece)
     dpre_mine, dpre_sent = hidden_gradient(core, piece, down_full, slopes, fscale)
@@ -306,7 +291,7 @@
     sums_up = from_axis(blocks_up, "x", rows_down)
     rows_up = from_axis(sums_up, "y")
     chip_rows = jnp.stack([rows_up, rows_down])
-    loss_total, square_total = totals(loss_part, rows_up, rows_down)
+    square_total = total(jnp.sum(rows_up * rows_up + rows_down * rows_down))
     by_core = chip_rows.reshape(2, 2, blocks[2] // 2, -1)
     kept = lax.dynamic_index_in_dim(by_core, core, 1, keepdims=False)
     other = core_swapped(lax.dynamic_index_in_dim(by_core, 1 - core, 1, keepdims=False))
@@ -315,11 +300,12 @@
     )
     clip_limit = math.sqrt(2.0 * width_full * hidden_local * lax.axis_size("mp"))
     factor = clip_limit / jnp.maximum(jnp.sqrt(square_total), clip_limit)
+    factor = jnp.tile(factor, (1, hidden_local // factor.shape[1]))
     new_up, up_m, up_v = adam_update(up_master, up_moment, up_second, mine_up, factor)
     new_down, down_m, down_v = adam_update(
         down_master, down_moment, down_second, mine_down, factor
     )
-    loss_mean = loss_total / (sample_total * token_count * width_full)
+    loss_mean = loss_total[0, 0] / (sample_total * token_count * width_full)
     return (new_up, new_down, up_m, down_m, up_v, down_v, loss_mean)
 
 

time: 268 us -> 266 us (level)
  waiting for transfers between devices: 132 us -> 106 us
  blocking collectives: 37.1 us -> 60.9 us
  starting transfers between devices: 25.6 us -> 29.6 us
    all_to_all x0 -> x1, blocking collectives: none -> 23.8 us  [total(): rows = lax.all_to_all(rows, DP_MP, split_axis=0, concat_axis=0, tiled=True)]
    all_gather x1, waiting for transfers between devices: 42.7 us -> 20.9 us  [per_device(): lax.all_gather(dpred, 'mp', axis=0, tiled=True)]
    ppermute x12, waiting for transfers between devices: 28.1 us -> 24 us  [from_axis(): lax.ppermute(sent.astype(jnp.bfloat16), axis, [(i, (i + step) % size) for...]
    ppermute x12, starting transfers between devices: 15.8 us -> 19.2 us  [from_axis(): lax.ppermute(sent.astype(jnp.bfloat16), axis, [(i, (i + step) % size) for...]
  transfers between devices with their start and end apart: 22 -> 22, of which waited for: 13 -> 14; matrix products, arithmetic and copies ran while one was open for 8% -> 9% of each run, Pallas kernels for 4% -> 3%
where the time goes in v5:
time: 266 us; the launch traced here: 263 us
  waiting for transfers between devices  106 us (40%)
  blocking collectives  60.9 us (23%)
  starting transfers between devices  29.6 us (11%)
  Pallas kernels  20.7 us (8%)
  between operations  15.3 us (6%)
  matrix products  12.7 us (5%)
  other arithmetic  11.6 us (4%)
  local copies, waits for them, and re-layouts  6.8 us (3%)
    reduce_scatter x1, waiting for transfers between devices, per_device(): lax.psum_scatter(partial_value, 'mp', scatter_dimension=0, tiled=True)  38.7 us
    all_to_all x1, blocking collectives, gathered_weights(): lax.all_to_all(jnp.broadcast_to(both, (chips,) + both.shape), PLANE, spli...  37.1 us
    ppermute x12, waiting for transfers between devices, from_axis(): lax.ppermute(sent.astype(jnp.bfloat16), axis, [(i, (i + step) % size) for...  24 us
    all_to_all x1, blocking collectives, total(): rows = lax.all_to_all(rows, DP_MP, split_axis=0, concat_axis=0, tiled=True)  23.8 us
    all_gather x1, waiting for transfers between devices, per_device(): lax.all_gather(dpred, 'mp', axis=0, tiled=True)  20.9 us
    ppermute x12, starting transfers between devices, from_axis(): lax.ppermute(sent.astype(jnp.bfloat16), axis, [(i, (i + step) % size) for...  19.2 us
    pallas_call x1, Pallas kernels, forward(): pl.pallas_call(functools.partial(forward_kernel, up_scale=up_scale, down_...  13.9 us
    all_to_all x1, waiting for transfers between devices, total(): rows = lax.all_to_all(rows, DP_MP, split_axis=0, concat_axis=0, tiled=True)  11.3 us
  transfers between devices with their start and end apart: 22, of which 14 were waited for; matrix products, arithmetic and copies ran while one was open for 9% of the time, Pallas kernels for 3%

profile of v5, /device:TPU:2, one launch (start us, length us, event | category | flops | bytes accessed | tf_op | source)
XLA Modules:
  0.0 263.4 jit_solution(2752249591018740319)
XLA Ops:
  10.6 37.1 %all_to_all.15 = bf16[16,96,768]{2,1,0:T(8,128)(2,1)S(1)} all-to-all(bf16[16,96,768]{2,1,0:T(8,128)(2,1)S(1)} %broadcast_in_dim.14), channel_id=1, replica_groups=mesh['y'=4,'x'=4,'c'=2,'mp'=8] {'y','x'}, dimensions={0} | all-to-all | bytes 4718592 | tf_op jit(solution)/shard_map/all_to_all | solution.py:41
  47.9 4.5 %collective-permute-done = bf16[16,96,768]{2,1,0:T(8,128)(2,1)} collective-permute-done((bf16[16,96,768]{2,1,0:T(8,128)(2,1)S(1)}, bf16[16,96,768]{2,1,0:T(8,128)(2,1)}, u32[]{:S(2)}, u32[]{:S(2)}) %collective-permute-start) | collective-permute-done | bytes 2359328 | tf_op jit(solution)/shard_map/ppermute | solution.py:26
  54.2 2.8 %maximum_select_fusion = (bf16[16,96,768]{2,1,0:T(8,128)(2,1)}, bf16[16,96,768]{2,1,0:T(8,128)(2,1)}) fusion(bf16[16,48,768]{2,1,0:T(8,128)(2,1)S(1)} %get-tuple-element.68, bf16[16,48,768]{2,1,0:T(8,128)(2,1)S(1)} %get-tuple-element.66, pred[]{:T(512)S(6)} %eq.18, bf16[16,48,768]{2,1,0:T(8,128)(2,1)S(1)} %get-tuple-element.65, ...), kind=kLoop, calls=%fused_computation.6 | loop fusion | flops 21233664 | bytes 9437185 | tf_op jit(solution)/shard_map/jit(_where)/select_n | solution.py:31
  58.4 13.9 %forward.1 = (bf16[1536,1024]{1,0:T(8,128)(2,1)}, bf16[1024,384]{1,0:T(8,128)(2,1)}, bf16[1024,384]{1,0:T(8,128)(2,1)}, f32[1024,768]{1,0:T(8,128)}, bf16[1536,1024]{1,0:T(8,128)(2,1)}) custom-call(s32[1]{0:T(128)} %bitcast.core, bf16[1536,1024]{1,0:T(8,128)(2,1)} %all-gather.3.cloned.1.call-done.gathered, bf16[1536,768]{1,0:T(8,128)(2,1)} %bitcast.110, ...), custom_call_target="tpu_custom_call" | custom-call | flops 4831838208 | bytes 18874368 | tf_op jit(solution)/shard_map/forward/pallas_call | solution.py:88
  74.7 5.0 %collective-permute-done.2 = bf16[1024,384]{1,0:T(8,128)(2,1)} collective-permute-done((bf16[1024,384]{1,0:T(8,128)(2,1)S(1)}, bf16[1024,384]{1,0:T(8,128)(2,1)}, u32[]{:S(2)}, u32[]{:S(2)}) %collective-permute-start.2) | collective-permute-done | bytes 786464 | tf_op jit(solution)/shard_map/ppermute | solution.py:26
  79.6 38.7 %reduce-scatter.2.cloned.1.call-done = bf16[192,1024]{1,0:T(8,128)(2,1)} async-done(((bf16[1536,1024]{1,0:T(8,128)(2,1)}), bf16[192,1024]{1,0:T(8,128)(2,1)}) %reduce-scatter.2.cloned.1.call-update) | async-done | bytes 393232 | tf_op jit(solution)/shard_map/reduce_scatter | solution.py:263
  118.3 1.9 multiply_convert_fusion
  122.7 23.8 %all_to_all.16 = f32[256,1,128]{2,1,0:T(1,128)S(1)} all-to-all(f32[256,1,128]{2,1,0:T(1,128)S(1)} %broadcast_in_dim.16), channel_id=1, replica_groups=mesh['y'=4,'x'=4,'c'=2,'mp'=8] {'y','x','c','mp'}, dimensions={0} | all-to-all | bytes 262144 | tf_op jit(solution)/shard_map/all_to_all | solution.py:170
  146.6 20.9 %all-gather.5.cloned.1.call-done.piece = bf16[1536,1024]{1,0:T(8,128)(2,1)} async-done(((bf16[192,1024]{1,0:T(8,128)(2,1)}), bf16[1536,1024]{1,0:T(8,128)(2,1)}) %all-gather.5.cloned.1.call-update) | async-done | bytes 3145744 | tf_op jit(solution)/shard_map/all_gather | solution.py:274
  167.5 6.8 %hidden_gradient.1 = (bf16[1024,384]{1,0:T(8,128)(2,1)}, bf16[1024,384]{1,0:T(8,128)(2,1)}) custom-call(s32[1]{0:T(128)} %bitcast.core, bf16[1536,1024]{1,0:T(8,128)(2,1)} %all-gather.5.cloned.1.call-done.piece, bf16[1536,768]{1,0:T(8,128)(2,1)} %bitcast.109, f32[1024,768]{1,0:T(8,128)} %get-tuple-element.41.slopes), custom_call_target="tpu_custom_call" | custom-call | flops 2415919104 | bytes 10223616 | tf_op jit(solution)/shard_map/hidden_gradient/pallas_call | solution.py:129
  174.8 3.1 %fusion.53 = f32[1536,384]{1,0:T(8,128)S(1)} fusion(bf16[1536,1024]{1,0:T(8,128)(2,1)S(1)} %copy-done.10, bf16[1024,384]{1,0:T(8,128)(2,1)} %get-tuple-element.42), kind=kOutput, calls=%fused_computation.100 | convolution fusion | flops 1207959552 | bytes 6291456 | tf_op jit(solution)/shard_map/dot_general | solution.py:284
  177.9 1.8 fusion.54
  179.8 3.9 %fusion.3 = bf16[1536,384]{1,0:T(8,128)(2,1)S(1)} fusion(f32[1536,384]{1,0:T(8,128)S(1)} %fusion.54, bf16[1536,1024]{1,0:T(8,128)(2,1)} %collective-permute-done.4, bf16[1024,384]{1,0:T(8,128)(2,1)} %collective-permute-done.2), kind=kOutput, calls=%fused_computation.5 | convolution fusion | flops 1209729024 | bytes 7471104 | tf_op jit(solution)/shard_map/dot_general | solution.py:281
  185.4 2.7 %collective-permute-start.6 = (bf16[4,96,384]{2,1,0:T(8,128)(2,1)S(1)}, bf16[4,96,384]{2,1,0:T(8,128)(2,1)S(1)}, u32[]{:S(2)}, u32[]{:S(2)}) collective-permute-start(bf16[4,96,384]{2,1,0:T(8,128)(2,1)S(1)} %get-tuple-element.75), channel_id=1, source_target_pairs={{0,128},{64,192},{128,0},{192,64},{1,129},{65,193},{129,1},{193,65... | collective-permute-start | bytes 884744 | tf_op jit(solution)/shard_map/ppermute | solution.py:161
  189.6 3.8 %fusion.2 = bf16[1536,384]{1,0:T(8,128)(2,1)S(1)} fusion(f32[1536,384]{1,0:T(8,128)S(1)} %fusion.53, bf16[1536,1024]{1,0:T(8,128)(2,1)} %collective-permute-done.1, bf16[1024,384]{1,0:T(8,128)(2,1)S(1)} %collective-permute-done.3), kind=kOutput, calls=%fused_computation.4 | convolution fusion | flops 1209729024 | bytes 7471104 | tf_op jit(solution)/shard_map/dot_general | solution.py:285
  194.1 7.3 %collective-permute-done.6 = bf16[4,96,384]{2,1,0:T(8,128)(2,1)S(1)} collective-permute-done((bf16[4,96,384]{2,1,0:T(8,128)(2,1)S(1)}, bf16[4,96,384]{2,1,0:T(8,128)(2,1)S(1)}, u32[]{:S(2)}, u32[]{:S(2)}) %collective-permute-start.6) | collective-permute-done | bytes 294944 | tf_op jit(solution)/shard_map/ppermute | solution.py:161
  203.6 3.3 %collective-permute-start.9 = (bf16[96,384]{1,0:T(8,128)(2,1)S(1)}, bf16[96,384]{1,0:T(8,128)(2,1)S(1)}, u32[]{:S(2)}, u32[]{:S(2)}) collective-permute-start(bf16[96,384]{1,0:T(8,128)(2,1)S(1)} %get-tuple-element.81), channel_id=1, source_target_pairs={{0,32},{16,48},{32,0},{48,16},{1,33},{17,49},{33,1},{49,17},{2,34}... | collective-permute-start | bytes 221192 | tf_op jit(solution)/shard_map/ppermute | solution.py:161
  207.2 2.3 collective-permute-start.12
  210.1 6.9 %collective-permute-done.11 = bf16[4,96,384]{2,1,0:T(8,128)(2,1)S(1)} collective-permute-done((bf16[4,96,384]{2,1,0:T(8,128)(2,1)S(1)}, bf16[4,96,384]{2,1,0:T(8,128)(2,1)S(1)}, u32[]{:S(2)}, u32[]{:S(2)}) %collective-permute-start.11) | collective-permute-done | bytes 294944 | tf_op jit(solution)/shard_map/ppermute | solution.py:161
  218.6 3.7 %collective-permute-done.13 = bf16[4,96,384]{2,1,0:T(8,128)(2,1)S(1)} collective-permute-done((bf16[4,96,384]{2,1,0:T(8,128)(2,1)S(1)}, bf16[4,96,384]{2,1,0:T(8,128)(2,1)S(1)}, u32[]{:S(2)}, u32[]{:S(2)}) %collective-permute-start.13) | collective-permute-done | bytes 294944 | tf_op jit(solution)/shard_map/ppermute | solution.py:161
  224.1 3.1 %collective-permute-start.15 = (bf16[96,384]{1,0:T(8,128)(2,1)S(1)}, bf16[96,384]{1,0:T(8,128)(2,1)S(1)}, u32[]{:S(2)}, u32[]{:S(2)}) collective-permute-start(bf16[96,384]{1,0:T(8,128)(2,1)S(1)} %get-tuple-element.78), channel_id=1, source_target_pairs={{0,128},{64,192},{128,0},{192,64},{1,129},{65,193},{129,1},{193,65... | collective-permute-start | bytes 221192 | tf_op jit(solution)/shard_map/ppermute | solution.py:161
  228.1 2.8 %collective-permute-done.15 = bf16[96,384]{1,0:T(8,128)(2,1)S(1)} collective-permute-done((bf16[96,384]{1,0:T(8,128)(2,1)S(1)}, bf16[96,384]{1,0:T(8,128)(2,1)S(1)}, u32[]{:S(2)}, u32[]{:S(2)}) %collective-permute-start.15) | collective-permute-done | bytes 73760 | tf_op jit(solution)/shard_map/ppermute | solution.py:161
  233.7 9.5 %all-to-all-start.2 = ((f32[256,1,128]{2,1,0:T(1,128)}), f32[256,1,128]{2,1,0:T(1,128)S(1)}, u32[]{:S(2)}, u32[]{:S(2)}) async-start(f32[256,1,128]{2,1,0:T(1,128)} %broadcast_in_dim.17), calls=%async_computation.3 | async-start | bytes 262144 | tf_op jit(solution)/shard_map/all_to_all | solution.py:170
  243.3 11.3 %all-to-all-done.2 = f32[256,1,128]{2,1,0:T(1,128)S(1)} async-done(((f32[256,1,128]{2,1,0:T(1,128)}), f32[256,1,128]{2,1,0:T(1,128)S(1)}, u32[]{:S(2)}, u32[]{:S(2)}) %all-to-all-start.2) | async-done | bytes 131104 | tf_op jit(solution)/shard_map/all_to_all | solution.py:170
  (97 shorter events, 27.3 us)
Async XLA Ops:
  7.2 51.2 %all-gather.3.cloned.1.call-start = ((), (), s32[]{:S(2)}) async-start(), calls=%async_computation.4 | async-start | bytes 3538944 | tf_op jit(solution)/shard_map/all_gather | solution.py:245
  10.3 108.0 %reduce-scatter.2.cloned.1.call-start = ((), (), s32[]{:S(2)}) async-start(), calls=%async_computation.5 | async-start | bytes 3538944 | tf_op jit(solution)/shard_map/reduce_scatter | solution.py:263
  47.7 4.7 %collective-permute-start = (bf16[16,96,768]{2,1,0:T(8,128)(2,1)S(1)}, bf16[16,96,768]{2,1,0:T(8,128)(2,1)}, u32[]{:S(2)}, u32[]{:S(2)}) collective-permute-start(bf16[16,96,768]{2,1,0:T(8,128)(2,1)S(1)} %all_to_all.15), channel_id=1, source_target_pairs={{0,8},{8,0},{1,9},{9,1},{2,10},{10,2},{3,11},{11,3},{4,12},{12,4},... | collective-permute-start | bytes 7077896 | tf_op jit(solution)/shard_map/ppermute | solution.py:26
  72.4 95.1 %all-gather.5.cloned.1.call-start = ((), (), s32[]{:S(2)}) async-start(), calls=%async_computation.6 | async-start | bytes 3538944 | tf_op jit(solution)/shard_map/all_gather | solution.py:274
  72.4 7.2 %collective-permute-start.1 = (bf16[1536,1024]{1,0:T(8,128)(2,1)}, bf16[1536,1024]{1,0:T(8,128)(2,1)}, u32[]{:S(2)}, u32[]{:S(2)}) collective-permute-start(bf16[1536,1024]{1,0:T(8,128)(2,1)} %get-tuple-element.29), channel_id=1, source_target_pairs={{0,8},{8,0},{1,9},{9,1},{2,10},{10,2},{3,11},{11,3},{4,12},{12,4},... | collective-permute-start | bytes 9437192 | tf_op jit(solution)/shard_map/ppermute | solution.py:26
  73.4 6.2 %collective-permute-start.2 = (bf16[1024,384]{1,0:T(8,128)(2,1)S(1)}, bf16[1024,384]{1,0:T(8,128)(2,1)}, u32[]{:S(2)}, u32[]{:S(2)}) collective-permute-start(bf16[1024,384]{1,0:T(8,128)(2,1)S(1)} %copy-done.12), channel_id=1, source_target_pairs={{0,8},{8,0},{1,9},{9,1},{2,10},{10,2},{3,11},{11,3},{4,12},{12,4},... | collective-permute-start | bytes 2359304 | tf_op jit(solution)/shard_map/ppermute | solution.py:26
  167.5 12.3 %collective-permute-start.4 = (bf16[1536,1024]{1,0:T(8,128)(2,1)}, bf16[1536,1024]{1,0:T(8,128)(2,1)}, u32[]{:S(2)}, u32[]{:S(2)}) collective-permute-start(bf16[1536,1024]{1,0:T(8,128)(2,1)} %all-gather.5.cloned.1.call-done.piece), channel_id=1, source_target_pairs={{0,8},{8,0},{1,9},{9,1},{2,10},{10,2},{3,11},{11,3},{4,12},{12,4},... | collective-permute-start | bytes 9437192 | tf_op jit(solution)/shard_map/ppermute | solution.py:26
  174.3 15.3 %collective-permute-start.3 = (bf16[1024,384]{1,0:T(8,128)(2,1)}, bf16[1024,384]{1,0:T(8,128)(2,1)S(1)}, u32[]{:S(2)}, u32[]{:S(2)}) collective-permute-start(bf16[1024,384]{1,0:T(8,128)(2,1)} %get-tuple-element.44), channel_id=1, source_target_pairs={{0,8},{8,0},{1,9},{9,1},{2,10},{10,2},{3,11},{11,3},{4,12},{12,4},... | collective-permute-start | bytes 2359304 | tf_op jit(solution)/shard_map/ppermute | solution.py:26
  183.8 10.2 %collective-permute-start.5 = (bf16[4,96,384]{2,1,0:T(8,128)(2,1)S(1)}, bf16[4,96,384]{2,1,0:T(8,128)(2,1)S(1)}, u32[]{:S(2)}, u32[]{:S(2)}) collective-permute-start(bf16[4,96,384]{2,1,0:T(8,128)(2,1)S(1)} %get-tuple-element.73), channel_id=1, source_target_pairs={{0,64},{64,128},{128,192},{192,0},{1,65},{65,129},{129,193},{193,1... | collective-permute-start | bytes 884744 | tf_op jit(solution)/shard_map/ppermute | solution.py:161
  185.4 16.0 %collective-permute-start.6 = (bf16[4,96,384]{2,1,0:T(8,128)(2,1)S(1)}, bf16[4,96,384]{2,1,0:T(8,128)(2,1)S(1)}, u32[]{:S(2)}, u32[]{:S(2)}) collective-permute-start(bf16[4,96,384]{2,1,0:T(8,128)(2,1)S(1)} %get-tuple-element.75), channel_id=1, source_target_pairs={{0,128},{64,192},{128,0},{192,64},{1,129},{65,193},{129,1},{193,65... | collective-permute-start | bytes 884744 | tf_op jit(solution)/shard_map/ppermute | solution.py:161
  188.1 13.2 %collective-permute-start.7 = (bf16[4,96,384]{2,1,0:T(8,128)(2,1)S(1)}, bf16[4,96,384]{2,1,0:T(8,128)(2,1)S(1)}, u32[]{:S(2)}, u32[]{:S(2)}) collective-permute-start(bf16[4,96,384]{2,1,0:T(8,128)(2,1)S(1)} %get-tuple-element.74), channel_id=1, source_target_pairs={{0,192},{64,0},{128,64},{192,128},{1,193},{65,1},{129,65},{193,129... | collective-permute-start | bytes 884744 | tf_op jit(solution)/shard_map/ppermute | solution.py:161
  201.5 7.9 %collective-permute-start.10 = (bf16[96,384]{1,0:T(8,128)(2,1)S(1)}, bf16[96,384]{1,0:T(8,128)(2,1)S(1)}, u32[]{:S(2)}, u32[]{:S(2)}) collective-permute-start(bf16[96,384]{1,0:T(8,128)(2,1)S(1)} %get-tuple-element.80), channel_id=1, source_target_pairs={{0,48},{16,0},{32,16},{48,32},{1,49},{17,1},{33,17},{49,33},{2,50}... | collective-permute-start | bytes 221192 | tf_op jit(solution)/shard_map/ppermute | solution.py:161
  202.2 7.9 %collective-permute-start.8 = (bf16[96,384]{1,0:T(8,128)(2,1)S(1)}, bf16[96,384]{1,0:T(8,128)(2,1)S(1)}, u32[]{:S(2)}, u32[]{:S(2)}) collective-permute-start(bf16[96,384]{1,0:T(8,128)(2,1)S(1)} %get-tuple-element.79), channel_id=1, source_target_pairs={{0,16},{16,32},{32,48},{48,0},{1,17},{17,33},{33,49},{49,1},{2,18}... | collective-permute-start | bytes 221192 | tf_op jit(solution)/shard_map/ppermute | solution.py:161
  203.6 6.4 %collective-permute-start.9 = (bf16[96,384]{1,0:T(8,128)(2,1)S(1)}, bf16[96,384]{1,0:T(8,128)(2,1)S(1)}, u32[]{:S(2)}, u32[]{:S(2)}) collective-permute-start(bf16[96,384]{1,0:T(8,128)(2,1)S(1)} %get-tuple-element.81), channel_id=1, source_target_pairs={{0,32},{16,48},{32,0},{48,16},{1,33},{17,49},{33,1},{49,17},{2,34}... | collective-permute-start | bytes 221192 | tf_op jit(solution)/shard_map/ppermute | solution.py:161
  207.1 10.0 %collective-permute-start.11 = (bf16[4,96,384]{2,1,0:T(8,128)(2,1)S(1)}, bf16[4,96,384]{2,1,0:T(8,128)(2,1)S(1)}, u32[]{:S(2)}, u32[]{:S(2)}) collective-permute-start(bf16[4,96,384]{2,1,0:T(8,128)(2,1)S(1)} %get-tuple-element.69), channel_id=1, source_target_pairs={{0,16},{16,32},{32,48},{48,0},{1,17},{17,33},{33,49},{49,1},{2,18}... | collective-permute-start | bytes 884744 | tf_op jit(solution)/shard_map/ppermute | solution.py:161
  207.2 11.5 %collective-permute-start.12 = (bf16[4,96,384]{2,1,0:T(8,128)(2,1)S(1)}, bf16[4,96,384]{2,1,0:T(8,128)(2,1)S(1)}, u32[]{:S(2)}, u32[]{:S(2)}) collective-permute-start(bf16[4,96,384]{2,1,0:T(8,128)(2,1)S(1)} %get-tuple-element.71), channel_id=1, source_target_pairs={{0,32},{16,48},{32,0},{48,16},{1,33},{17,49},{33,1},{49,17},{2,34}... | collective-permute-start | bytes 884744 | tf_op jit(solution)/shard_map/ppermute | solution.py:161
  209.5 12.9 %collective-permute-start.13 = (bf16[4,96,384]{2,1,0:T(8,128)(2,1)S(1)}, bf16[4,96,384]{2,1,0:T(8,128)(2,1)S(1)}, u32[]{:S(2)}, u32[]{:S(2)}) collective-permute-start(bf16[4,96,384]{2,1,0:T(8,128)(2,1)S(1)} %get-tuple-element.70), channel_id=1, source_target_pairs={{0,48},{16,0},{32,16},{48,32},{1,49},{17,1},{33,17},{49,33},{2,50}... | collective-permute-start | bytes 884744 | tf_op jit(solution)/shard_map/ppermute | solution.py:161
  210.1 44.6 %copy-start.6 = (f32[48,768]{1,0:T(8,128)S(1)}, f32[48,768]{1,0:T(8,128)}, u32[]{:S(2)}) copy-start(f32[48,768]{1,0:T(8,128)} %param.21) | copy-start | bytes 442372
  210.1 44.6 %copy-start.7 = (f32[48,768]{1,0:T(8,128)S(1)}, f32[48,768]{1,0:T(8,128)}, u32[]{:S(2)}) copy-start(f32[48,768]{1,0:T(8,128)} %param.23) | copy-start | bytes 442372
  222.5 5.7 %collective-permute-start.14 = (bf16[96,384]{1,0:T(8,128)(2,1)S(1)}, bf16[96,384]{1,0:T(8,128)(2,1)S(1)}, u32[]{:S(2)}, u32[]{:S(2)}) collective-permute-start(bf16[96,384]{1,0:T(8,128)(2,1)S(1)} %get-tuple-element.76), channel_id=1, source_target_pairs={{0,64},{64,128},{128,192},{192,0},{1,65},{65,129},{129,193},{193,1... | collective-permute-start | bytes 221192 | tf_op jit(solution)/shard_map/ppermute | solution.py:161
  224.1 6.8 %collective-permute-start.15 = (bf16[96,384]{1,0:T(8,128)(2,1)S(1)}, bf16[96,384]{1,0:T(8,128)(2,1)S(1)}, u32[]{:S(2)}, u32[]{:S(2)}) collective-permute-start(bf16[96,384]{1,0:T(8,128)(2,1)S(1)} %get-tuple-element.78), channel_id=1, source_target_pairs={{0,128},{64,192},{128,0},{192,64},{1,129},{65,193},{129,1},{193,65... | collective-permute-start | bytes 221192 | tf_op jit(solution)/shard_map/ppermute | solution.py:161
  227.2 4.4 %collective-permute-start.16 = (bf16[96,384]{1,0:T(8,128)(2,1)S(1)}, bf16[96,384]{1,0:T(8,128)(2,1)S(1)}, u32[]{:S(2)}, u32[]{:S(2)}) collective-permute-start(bf16[96,384]{1,0:T(8,128)(2,1)S(1)} %get-tuple-element.77), channel_id=1, source_target_pairs={{0,192},{64,0},{128,64},{192,128},{1,193},{65,1},{129,65},{193,129... | collective-permute-start | bytes 221192 | tf_op jit(solution)/shard_map/ppermute | solution.py:161
  232.2 11.0 %collective-permute-start.17 = (f32[2,48,384]{2,1,0:T(8,128)S(1)}, f32[2,48,384]{2,1,0:T(8,128)S(1)}, u32[]{:S(2)}, u32[]{:S(2)}) collective-permute-start(f32[2,48,384]{2,1,0:T(8,128)S(1)} %get-tuple-element.86), channel_id=1, source_target_pairs={{0,8},{8,0},{1,9},{9,1},{2,10},{10,2},{3,11},{11,3},{4,12},{12,4},... | collective-permute-start | bytes 442376 | tf_op jit(solution)/shard_map/ppermute | solution.py:26
  233.7 20.9 %all-to-all-start.2 = ((f32[256,1,128]{2,1,0:T(1,128)}), f32[256,1,128]{2,1,0:T(1,128)S(1)}, u32[]{:S(2)}, u32[]{:S(2)}) async-start(f32[256,1,128]{2,1,0:T(1,128)} %broadcast_in_dim.17), calls=%async_computation.3 | async-start | bytes 262144 | tf_op jit(solution)/shard_map/all_to_all | solution.py:170
  (12 other events, 115.7 us)
Sparse Core Ops, SparseCore 0:
  10.4 47.9 all-gather.2
  72.5 45.7 reduce-scatter.1
  120.3 47.1 all-gather.4
